TPU v7x, 32 devices: a whole 2x2x4 slice. The times are simulated.
32 devices in a mesh: dp: 8 (over z, core), row: 2 (over x), col: 2 (over y).
Axes of the slice: x: 2, y: 2, z: 4, core: 2. Of those that a mesh axis runs over, the one named last changes fastest.
Arguments:
- tokens: bfloat16 [4096, 8192], P(('dp', 'row', 'col')), parts along dimension 0, may hold values from -6 to 6
- w_gate: bfloat16 [8192, 1024], P(('row', 'col')), may hold values from -0.0625 to 0.0625
- w_up: bfloat16 [8192, 1024], P(('row', 'col')), may hold values from -0.0625 to 0.0625
- w_down: bfloat16 [1024, 8192], P(None, ('row', 'col')), may hold values from -0.1875 to 0.1875
Outputs:
- mixed: bfloat16 [4096, 8192], P(('dp', 'row', 'col')), parts along dimension 0
There are 8 independent parts, one for each index of `dp`. A program takes and returns all parts, laid end to end along the dimension named above; an argument that names none is the same for every part. Nothing has to cross between parts.
All inputs are finite; a program needn't handle non-finite values.
Results may differ from a plain program's by a relative error of at most 0.029.
Values may be sent and summed in bfloat16 or wider, within the bound.
No kernel may reach another device: no remote copies, remote signals or barrier semaphores. Data moves between devices by JAX's collectives and lax.ppermute only.
A program may use at most 64 MiB of HBM per device.

v0:
```python
import jax
import jax.numpy as jnp
from jax import lax
from jax.sharding import PartitionSpec as P


def solution(mesh):
    rows, cols, dp = mesh.shape["row"], mesh.shape["col"], mesh.shape["dp"]
    cores = 2 if dp % 2 == 0 else 1
    chips = dp // cores
    turned = cores == 2 and rows == cols
    line = turned and chips == 4
    count_a, count_b = cols, rows
    shifts = [(a, b) for a in range(count_a) for b in range(count_b)]
    away = [s for s in shifts if s != (0, 0)]

    def send(x, shift):
        pairs = []
        for d in range(dp):
            dr, dc = shift if turned and d % cores else shift[::-1]
            for r in range(rows):
                for c in range(cols):
                    to = (d * rows + (r + dr) % rows) * cols + (c + dc) % cols
                    pairs.append(((d * rows + r) * cols + c, to))
        return lax.ppermute(x, ("dp", "row", "col"), pairs)

    def send_dp(x, chip_pairs, core_shift):
        pairs = [(z * cores + k, to * cores + (k + core_shift) % cores) for z, to in chip_pairs for k in range(cores)]
        return lax.ppermute(x, "dp", pairs)

    def matmul(x, y):
        return jnp.dot(x, y, preferred_element_type=jnp.float32)

    def shards(tokens, w_gate, w_up, w_down):
        r, c, d = lax.axis_index("row"), lax.axis_index("col"), lax.axis_index("dp")
        chip, core = d // cores, d % cores
        slab = w_gate.shape[0]
        hidden_width, width = w_down.shape
        half = width // 2
        at_b = core * half if turned else 0
        at_a = half - at_b

        def place(a, b):
            dr, dc = (b + core * (a - b), a + core * (b - a)) if turned else (b, a)
            return (r + dr) % rows * cols + (c + dc) % cols

        def columns(x, at, size):
            return lax.dynamic_slice_in_dim(x, at, size, axis=1)

        early, late = [], []
        if turned:
            share = hidden_width // chips
            piece = lax.dynamic_slice(w_down, (chip * share, at_b), (share, half))
            held = [send(piece, (-a, 0)) for a in range(1, count_a)]
            held = held[0] if len(held) == 1 else jnp.concatenate(held, axis=0)

        feats = {s: columns(tokens, place(*s) * slab, slab) for s in shifts}
        got = {s: send(feats[s], s) for s in away}
        got[0, 0] = feats[0, 0]

        if line:
            two = send_dp(held, [(z, z ^ 2) for z in range(chips)], 0)
            one = send_dp(held, [(z, z ^ 1) for z in range(chips)], 0)
            middle = send_dp(held, [(1, 2), (2, 1)], 0)
            early += [(one, chip ^ 1), (two, chip ^ 2)]
        elif turned:
            for z in range(1, chips):
                turn = send_dp(held, [(i, (i + z) % chips) for i in range(chips)], 0)
                late.append((turn, (chip - z) % chips))

        def crossed(weight, a_first):
            first, second = (count_a, count_b) if a_first else (count_b, count_a)

            def shift(i, j):
                return (i, j) if a_first else (j, i)

            parts = {s: matmul(got[s], weight) for s in away}
            parts[0, 0] = matmul(got[0, 0], weight)
            sums = {j: parts[shift(0, j)] for j in range(second)}
            for j in reversed(range(second)):
                for i in range(1, first):
                    part = send(parts[shift(i, j)].astype(jnp.bfloat16), shift(-i, 0))
                    sums[j] = sums[j] + part.astype(jnp.float32)
            total = sums[0]
            passed = [sums[j].astype(jnp.bfloat16) for j in range(1, second)]
            for j in range(1, second):
                total = total + send(passed[j - 1], shift(0, -j)).astype(jnp.float32)
            return total, passed

        gate, gate_passed = crossed(w_gate, True)
        up, up_passed = crossed(w_up, False)
        hidden = (jax.nn.silu(gate) * up).astype(jnp.bfloat16)

        if turned:
            if line:
                relayed = send_dp(two, [(2, 3), (1, 0)], 0)
                late.append((jnp.where((chip == 0) | (chip == chips - 1), relayed, middle), chip ^ 3))
            far_b = {a: jnp.zeros((hidden_width, half), jnp.bfloat16) for a in range(1, count_a)}
            far_a = {b: jnp.zeros((hidden_width, half), jnp.bfloat16) for b in range(1, count_b)}

            def fill(far, block, from_chip):
                for i in far:
                    rows_of = block[(i - 1) * share : i * share]
                    far[i] = lax.dynamic_update_slice_in_dim(far[i], rows_of, from_chip * share, axis=0)

            def fill_both(pieces):
                for block, from_chip in pieces:
                    fill(far_b, block, from_chip)
                for block, from_chip in pieces:
                    fill(far_a, send_dp(block, [(z, z) for z in range(chips)], 1), from_chip)

            fill_both([(held, chip)])
            tied, _ = lax.optimization_barrier(([p for p, _ in early], gate_passed + up_passed))
            fill_both([(p, at) for p, (_, at) in zip(tied, early)])
        else:
            far_b = {a: send(w_down[:, :half], (-a, 0)) for a in range(1, count_a)}
            far_a = {b: send(w_down[:, half:], (0, -b)) for b in range(1, count_b)}

        near_b = {b: send(hidden, (0, -b)) for b in range(1, count_b)}
        near_a = {a: send(hidden, (-a, 0)) for a in range(1, count_a)}
        w_b, w_a = columns(w_down, at_b, half), columns(w_down, at_a, half)

        outs = []

        def give(x, weight, shift, slab_from, at):
            out = send(matmul(x, weight).astype(jnp.bfloat16), shift)
            outs.append((out, place(*slab_from) * width + at))

        for b, other in near_b.items():
            give(other, w_b, (0, b), (0, -b), at_b)
        for a, other in near_a.items():
            give(other, w_a, (a, 0), (-a, 0), at_a)
        if turned:
            tied, _ = lax.optimization_barrier(([p for p, _ in late], hidden))
            fill_both([(p, at) for p, (_, at) in zip(tied, late)])
        for b, other in near_b.items():
            for a in far_b:
                give(other, far_b[a], (0, b), (a, -b), at_b)
        for a, other in near_a.items():
            for b in far_a:
                give(other, far_a[b], (a, 0), (-a, b), at_a)

        landed = [(matmul(hidden, w_down).astype(jnp.bfloat16), place(0, 0) * width)]
        for a in far_b:
            landed.append((matmul(hidden, far_b[a]).astype(jnp.bfloat16), place(a, 0) * width + at_b))
        for b in far_a:
            landed.append((matmul(hidden, far_a[b]).astype(jnp.bfloat16), place(0, b) * width + at_a))
        mixed = jnp.zeros((tokens.shape[0], width * rows * cols), jnp.bfloat16)
        for block, at in landed + outs:
            mixed = lax.dynamic_update_slice_in_dim(mixed, block, at, axis=1)
        return mixed

    in_specs = (
        P(("dp", "row", "col"), None),
        P(("row", "col"), None),
        P(("row", "col"), None),
        P(None, ("row", "col")),
    )
    out_specs = P(("dp", "row", "col"), None)
    return jax.shard_map(shards, mesh=mesh, in_specs=in_specs, out_specs=out_specs, check_vma=False)
```

profile of v0, /device:TPU:0, one launch (start us, length us, event | category | flops | bytes accessed | tf_op | source)
XLA Modules:
  0.0 101.6 jit_solution(1140664525421565601)
XLA Ops:
  0.0 2.7 %constant_dynamic-slice_fusion.1 = (bf16[128,2048]{1,0:T(8,128)(2,1)}, bf16[128,2048]{1,0:T(8,128)(2,1)}, bf16[128,2048]{1,0:T(8,128)(2,1)}) fusion(bf16[128,8192]{1,0:T(8,128)(2,1)} %param.4, s32[]{:T(128)S(6)} %select_n.159, s32[]{:T(128)S(6)} %select_n.156, s32[]{:T(128)S(6)} %select_n.162), kind=kLoop, calls=%fused_computation.44 | loop fusion | bytes 3145740 | tf_op jit(solution)/shard_map/dynamic_slice | solution.py:48
  2.7 3.9 %collective-permute-start.3 = (bf16[128,2048]{1,0:T(8,128)(2,1)}, bf16[128,2048]{1,0:T(8,128)(2,1)}, u32[]{:S(2)}, u32[]{:S(2)}) collective-permute-start(bf16[128,2048]{1,0:T(8,128)(2,1)} %get-tuple-element.13), channel_id=1, source_target_pairs={{0,3},{1,2},{2,1},{3,0},{4,7},{5,6},{6,5},{7,4},{8,11},{9,10},{10,... | collective-permute-start | bytes 1572872 | tf_op jit(solution)/shard_map/ppermute | solution.py:25
  7.2 1.9 %dynamic_slice.25 = bf16[256,1024]{1,0:T(8,128)(2,1)} dynamic-slice(bf16[1024,2048]{1,0:T(8,128)(2,1)} %param.7, s32[]{:T(128)S(6)} %select_n.164, s32[]{:T(128)S(6)} %select_n.165), dynamic_slice_sizes={256,1024} | dynamic-slice | bytes 1048580 | tf_op jit(solution)/shard_map/dynamic_slice | solution.py:53
  9.1 2.0 %collective-permute-start.9 = (bf16[256,1024]{1,0:T(8,128)(2,1)}, bf16[256,1024]{1,0:T(8,128)(2,1)}, u32[]{:S(2)}, u32[]{:S(2)}) collective-permute-start(bf16[256,1024]{1,0:T(8,128)(2,1)} %dynamic_slice.25), channel_id=1, source_target_pairs={{0,1},{1,0},{2,3},{3,2},{4,6},{5,7},{6,4},{7,5},{8,9},{9,8},{10,11... | collective-permute-start | bytes 1572872 | tf_op jit(solution)/shard_map/ppermute | solution.py:25
  11.1 3.9 %fusion.15 = f32[128,1024]{1,0:T(8,128)} fusion(bf16[2048,1024]{1,0:T(8,128)(2,1)} %param.6, bf16[128,8192]{1,0:T(8,128)(2,1)S(1)} %copy-done.3, s32[]{:T(128)S(6)} %select_n.152), kind=kOutput, calls=%fused_computation.24 | convolution fusion | flops 536870912 | bytes 5242884 | tf_op jit(solution)/shard_map/dot_general | solution.py:32
  14.9 4.8 %collective-permute-done.3 = bf16[128,2048]{1,0:T(8,128)(2,1)} collective-permute-done((bf16[128,2048]{1,0:T(8,128)(2,1)}, bf16[128,2048]{1,0:T(8,128)(2,1)}, u32[]{:S(2)}, u32[]{:S(2)}) %collective-permute-start.3) | collective-permute-done | bytes 524320 | tf_op jit(solution)/shard_map/ppermute | solution.py:25
  19.8 1.8 %convolution_convert_fusion.7 = bf16[128,1024]{1,0:T(8,128)(2,1)S(1)} fusion(bf16[128,2048]{1,0:T(8,128)(2,1)} %collective-permute-done.3, bf16[2048,1024]{1,0:T(8,128)(2,1)S(1)} %copy-done.1), kind=kOutput, calls=%fused_computation.20 | convolution fusion | flops 537001984 | bytes 4980736 | tf_op jit(solution)/shard_map/dot_general | solution.py:32
  21.6 2.1 %collective-permute-start.4 = (bf16[128,1024]{1,0:T(8,128)(2,1)S(1)}, bf16[128,1024]{1,0:T(8,128)(2,1)S(1)}, u32[]{:S(2)}, u32[]{:S(2)}) collective-permute-start(bf16[128,1024]{1,0:T(8,128)(2,1)S(1)} %convolution_convert_fusion.7), channel_id=1, source_target_pairs={{0,1},{1,0},{2,3},{3,2},{4,6},{5,7},{6,4},{7,5},{8,9},{9,8},{10,11... | collective-permute-start | bytes 786440 | tf_op jit(solution)/shard_map/ppermute | solution.py:25
  23.6 1.8 %convolution_convert_fusion.5 = bf16[128,1024]{1,0:T(8,128)(2,1)S(1)} fusion(bf16[128,2048]{1,0:T(8,128)(2,1)} %collective-permute-done.3, bf16[2048,1024]{1,0:T(8,128)(2,1)S(1)} %copy-done), kind=kOutput, calls=%fused_computation.18 | convolution fusion | flops 537001984 | bytes 4980736 | tf_op jit(solution)/shard_map/dot_general | solution.py:32
  25.4 1.5 %collective-permute-start.7 = (bf16[128,1024]{1,0:T(8,128)(2,1)S(1)}, bf16[128,1024]{1,0:T(8,128)(2,1)S(1)}, u32[]{:S(2)}, u32[]{:S(2)}) collective-permute-start(bf16[128,1024]{1,0:T(8,128)(2,1)S(1)} %convolution_convert_fusion.5), channel_id=1, source_target_pairs={{0,2},{1,3},{2,0},{3,1},{4,5},{5,4},{6,7},{7,6},{8,10},{9,11},{10,... | collective-permute-start | bytes 786440 | tf_op jit(solution)/shard_map/ppermute | solution.py:25
  27.0 3.1 %collective-permute-done = bf16[128,2048]{1,0:T(8,128)(2,1)S(1)} collective-permute-done((bf16[128,2048]{1,0:T(8,128)(2,1)}, bf16[128,2048]{1,0:T(8,128)(2,1)S(1)}, u32[]{:S(2)}, u32[]{:S(2)}) %collective-permute-start) | collective-permute-done | bytes 524320 | tf_op jit(solution)/shard_map/ppermute | solution.py:25
  30.9 1.8 %collective-permute-start.1 = (bf16[128,1024]{1,0:T(8,128)(2,1)S(1)}, bf16[128,1024]{1,0:T(8,128)(2,1)S(1)}, u32[]{:S(2)}, u32[]{:S(2)}) collective-permute-start(bf16[128,1024]{1,0:T(8,128)(2,1)S(1)} %convolution_convert_fusion.8), channel_id=1, source_target_pairs={{0,1},{1,0},{2,3},{3,2},{4,6},{5,7},{6,4},{7,5},{8,9},{9,8},{10,11... | collective-permute-start | bytes 786440 | tf_op jit(solution)/shard_map/ppermute | solution.py:25
  32.6 1.4 %convolution_convert_fusion.6 = bf16[128,1024]{1,0:T(8,128)(2,1)} fusion(bf16[128,2048]{1,0:T(8,128)(2,1)S(1)} %collective-permute-done.2, bf16[2048,1024]{1,0:T(8,128)(2,1)S(1)} %copy-done), kind=kOutput, calls=%fused_computation.19 | convolution fusion | flops 537001984 | bytes 4980736 | tf_op jit(solution)/shard_map/dot_general | solution.py:32
  34.1 1.5 %collective-permute-start.6 = (bf16[128,1024]{1,0:T(8,128)(2,1)}, bf16[128,1024]{1,0:T(8,128)(2,1)}, u32[]{:S(2)}, u32[]{:S(2)}) collective-permute-start(bf16[128,1024]{1,0:T(8,128)(2,1)} %convolution_convert_fusion.6), channel_id=1, source_target_pairs={{0,2},{1,3},{2,0},{3,1},{4,5},{5,4},{6,7},{7,6},{8,10},{9,11},{10,... | collective-permute-start | bytes 786440 | tf_op jit(solution)/shard_map/ppermute | solution.py:25
  35.6 5.8 %collective-permute-done.9 = bf16[256,1024]{1,0:T(8,128)(2,1)} collective-permute-done((bf16[256,1024]{1,0:T(8,128)(2,1)}, bf16[256,1024]{1,0:T(8,128)(2,1)}, u32[]{:S(2)}, u32[]{:S(2)}) %collective-permute-start.9) | collective-permute-done | bytes 524320 | tf_op jit(solution)/shard_map/ppermute | solution.py:25
  41.3 1.8 %collective-permute-start.10 = (bf16[256,1024]{1,0:T(8,128)(2,1)}, bf16[256,1024]{1,0:T(8,128)(2,1)}, u32[]{:S(2)}, u32[]{:S(2)}) collective-permute-start(bf16[256,1024]{1,0:T(8,128)(2,1)} %collective-permute-done.9), channel_id=1, source_target_pairs={{0,8},{4,12},{8,0},{12,4},{16,24},{20,28},{24,16},{28,20},{1,9},{5... | collective-permute-start | bytes 1572872 | tf_op jit(solution)/shard_map/ppermute | solution.py:29
  44.1 2.8 %collective-permute-start.11 = (bf16[256,1024]{1,0:T(8,128)(2,1)}, bf16[256,1024]{1,0:T(8,128)(2,1)}, u32[]{:S(2)}, u32[]{:S(2)}) collective-permute-start(bf16[256,1024]{1,0:T(8,128)(2,1)} %collective-permute-done.9), channel_id=1, source_target_pairs={{0,16},{4,20},{8,24},{12,28},{16,0},{20,4},{24,8},{28,12},{1,17},{... | collective-permute-start | bytes 1572872 | tf_op jit(solution)/shard_map/ppermute | solution.py:29
  46.8 1.5 %fusion.13 = bf16[128,1024]{1,0:T(8,128)(2,1)} fusion(bf16[128,2048]{1,0:T(8,128)(2,1)S(1)} %collective-permute-done.2, bf16[2048,1024]{1,0:T(8,128)(2,1)S(1)} %copy-done.1, bf16[128,1024]{1,0:T(8,128)(2,1)S(1)} %collective-permute-done.4), kind=kOutput, calls=%fused_computation.16 | convolution fusion | flops 537264128 | bytes 5242880 | tf_op jit(solution)/shard_map/dot_general | solution.py:32
  48.3 1.5 %collective-permute-start.5 = (bf16[128,1024]{1,0:T(8,128)(2,1)}, bf16[128,1024]{1,0:T(8,128)(2,1)S(1)}, u32[]{:S(2)}, u32[]{:S(2)}) collective-permute-start(bf16[128,1024]{1,0:T(8,128)(2,1)} %fusion.13), channel_id=1, source_target_pairs={{0,2},{1,3},{2,0},{3,1},{4,5},{5,4},{6,7},{7,6},{8,10},{9,11},{10,... | collective-permute-start | bytes 786440 | tf_op jit(solution)/shard_map/ppermute | solution.py:25
  52.7 1.1 %constant_dynamic-update-slice_fusion.11 = bf16[1024,1024]{1,0:T(8,128)(2,1)S(1)} fusion(bf16[1024,1024]{1,0:T(8,128)(2,1)S(1)} %broadcast.23.clone, bf16[256,1024]{1,0:T(8,128)(2,1)} %collective-permute-done.9, s32[]{:T(128)S(6)} %select_n.164), kind=kLoop, calls=%fused_computation.42 | loop fusion | bytes 1048580 | tf_op jit(solution)/shard_map/dynamic_update_slice | solution.py:104
  53.9 3.6 %collective-permute-done.5 = bf16[128,1024]{1,0:T(8,128)(2,1)S(1)} collective-permute-done((bf16[128,1024]{1,0:T(8,128)(2,1)}, bf16[128,1024]{1,0:T(8,128)(2,1)S(1)}, u32[]{:S(2)}, u32[]{:S(2)}) %collective-permute-start.5) | collective-permute-done | bytes 262176 | tf_op jit(solution)/shard_map/ppermute | solution.py:25
  58.2 1.3 %multiply_convert_fusion = bf16[128,1024]{1,0:T(8,128)(2,1)S(1)} fusion(bf16[128,1024]{1,0:T(8,128)(2,1)} %collective-permute-done.8, f32[128,1024]{1,0:T(8,128)S(1)} %copy-done.5, bf16[128,1024]{1,0:T(8,128)(2,1)} %collective-permute-done.6, bf16[128,1024]{1,0:T(8,128)(2,1)S(1)} %collective-permute-done.5, f32[128,1024]{1,0:T(8,128)S(1)} %fusion.17, ...), kind=kLoop, calls=%fused_computation.22 | loop fusion | flops 1835008 | bytes 2359296 | tf_op jit(solution)/shard_map/convert_element_type | solution.py:92
  59.5 1.6 %collective-permute-start.20 = (bf16[128,1024]{1,0:T(8,128)(2,1)S(1)}, bf16[128,1024]{1,0:T(8,128)(2,1)S(1)}, u32[]{:S(2)}, u32[]{:S(2)}) collective-permute-start(bf16[128,1024]{1,0:T(8,128)(2,1)S(1)} %multiply_convert_fusion), channel_id=1, source_target_pairs={{0,1},{1,0},{2,3},{3,2},{4,6},{5,7},{6,4},{7,5},{8,9},{9,8},{10,11... | collective-permute-start | bytes 786440 | tf_op jit(solution)/shard_map/ppermute | solution.py:25
  61.7 1.5 %collective-permute-start.18 = (bf16[128,1024]{1,0:T(8,128)(2,1)S(1)}, bf16[128,1024]{1,0:T(8,128)(2,1)S(1)}, u32[]{:S(2)}, u32[]{:S(2)}) collective-permute-start(bf16[128,1024]{1,0:T(8,128)(2,1)S(1)} %multiply_convert_fusion), channel_id=1, source_target_pairs={{0,2},{1,3},{2,0},{3,1},{4,5},{5,4},{6,7},{7,6},{8,10},{9,11},{10,... | collective-permute-start | bytes 786440 | tf_op jit(solution)/shard_map/ppermute | solution.py:25
  63.2 8.1 %collective-permute-done.11 = bf16[256,1024]{1,0:T(8,128)(2,1)} collective-permute-done((bf16[256,1024]{1,0:T(8,128)(2,1)}, bf16[256,1024]{1,0:T(8,128)(2,1)}, u32[]{:S(2)}, u32[]{:S(2)}) %collective-permute-start.11) | collective-permute-done | bytes 524320 | tf_op jit(solution)/shard_map/ppermute | solution.py:29
  73.4 1.1 %constant_dynamic-update-slice_fusion.9 = bf16[1024,1024]{1,0:T(8,128)(2,1)S(1)} fusion(bf16[1024,1024]{1,0:T(8,128)(2,1)S(1)} %constant_dynamic-update-slice_fusion.10, bf16[256,1024]{1,0:T(8,128)(2,1)} %collective-permute-done.11, s32[]{:T(128)S(6)} %select_n.167), kind=kLoop, calls=%fused_computation.40 | loop fusion | bytes 1048580 | tf_op jit(solution)/shard_map/dynamic_update_slice | solution.py:104
  74.5 1.3 %collective-permute-start.12 = (bf16[256,1024]{1,0:T(8,128)(2,1)}, bf16[256,1024]{1,0:T(8,128)(2,1)S(1)}, u32[]{:S(2)}, u32[]{:S(2)}) collective-permute-start(bf16[256,1024]{1,0:T(8,128)(2,1)} %collective-permute-done.11), channel_id=1, source_target_pairs={{16,24},{20,28},{8,0},{12,4},{17,25},{21,29},{9,1},{13,5},{18,26},... | collective-permute-start | bytes 1572872 | tf_op jit(solution)/shard_map/ppermute | solution.py:29
  77.1 1.8 %collective-permute-start.19 = (bf16[128,1024]{1,0:T(8,128)(2,1)S(1)}, bf16[128,1024]{1,0:T(8,128)(2,1)S(1)}, u32[]{:S(2)}, u32[]{:S(2)}) collective-permute-start(bf16[128,1024]{1,0:T(8,128)(2,1)S(1)} %fusion.5), channel_id=1, source_target_pairs={{0,2},{1,3},{2,0},{3,1},{4,5},{5,4},{6,7},{7,6},{8,10},{9,11},{10,... | collective-permute-start | bytes 786440 | tf_op jit(solution)/shard_map/ppermute | solution.py:25
  80.1 10.9 %collective-permute-done.12 = bf16[256,1024]{1,0:T(8,128)(2,1)S(1)} collective-permute-done((bf16[256,1024]{1,0:T(8,128)(2,1)}, bf16[256,1024]{1,0:T(8,128)(2,1)S(1)}, u32[]{:S(2)}, u32[]{:S(2)}) %collective-permute-start.12) | collective-permute-done | bytes 524320 | tf_op jit(solution)/shard_map/ppermute | solution.py:29
  91.6 1.7 %collective-permute-start.22 = (bf16[128,1024]{1,0:T(8,128)(2,1)S(1)}, bf16[128,1024]{1,0:T(8,128)(2,1)S(1)}, u32[]{:S(2)}, u32[]{:S(2)}) collective-permute-start(bf16[128,1024]{1,0:T(8,128)(2,1)S(1)} %convolution_convert_fusion.2), channel_id=1, source_target_pairs={{0,2},{1,3},{2,0},{3,1},{4,5},{5,4},{6,7},{7,6},{8,10},{9,11},{10,... | collective-permute-start | bytes 786440 | tf_op jit(solution)/shard_map/ppermute | solution.py:25
  95.8 3.2 %collective-permute-done.22 = bf16[128,1024]{1,0:T(8,128)(2,1)S(1)} collective-permute-done((bf16[128,1024]{1,0:T(8,128)(2,1)S(1)}, bf16[128,1024]{1,0:T(8,128)(2,1)S(1)}, u32[]{:S(2)}, u32[]{:S(2)}) %collective-permute-start.22) | collective-permute-done | bytes 262176 | tf_op jit(solution)/shard_map/ppermute | solution.py:25
  99.0 1.9 %collective-permute-done.23 = bf16[128,1024]{1,0:T(8,128)(2,1)S(1)} collective-permute-done((bf16[128,1024]{1,0:T(8,128)(2,1)S(1)}, bf16[128,1024]{1,0:T(8,128)(2,1)S(1)}, u32[]{:S(2)}, u32[]{:S(2)}) %collective-permute-start.23) | collective-permute-done | bytes 262176 | tf_op jit(solution)/shard_map/ppermute | solution.py:25
  (62 shorter events, 14.4 us)
Async XLA Ops:
  0.0 11.1 %copy-start.3 = (bf16[128,8192]{1,0:T(8,128)(2,1)S(1)}, bf16[128,8192]{1,0:T(8,128)(2,1)}, u32[]{:S(2)}) copy-start(bf16[128,8192]{1,0:T(8,128)(2,1)} %param.4) | copy-start | bytes 6291460
  2.7 17.1 %collective-permute-start.3 = (bf16[128,2048]{1,0:T(8,128)(2,1)}, bf16[128,2048]{1,0:T(8,128)(2,1)}, u32[]{:S(2)}, u32[]{:S(2)}) collective-permute-start(bf16[128,2048]{1,0:T(8,128)(2,1)} %get-tuple-element.13), channel_id=1, source_target_pairs={{0,3},{1,2},{2,1},{3,0},{4,7},{5,6},{6,5},{7,4},{8,11},{9,10},{10,... | collective-permute-start | bytes 1572872 | tf_op jit(solution)/shard_map/ppermute | solution.py:25
  6.6 26.0 %collective-permute-start.2 = (bf16[128,2048]{1,0:T(8,128)(2,1)}, bf16[128,2048]{1,0:T(8,128)(2,1)S(1)}, u32[]{:S(2)}, u32[]{:S(2)}) collective-permute-start(bf16[128,2048]{1,0:T(8,128)(2,1)} %get-tuple-element.11), channel_id=1, source_target_pairs={{0,2},{1,3},{2,0},{3,1},{4,5},{5,4},{6,7},{7,6},{8,10},{9,11},{10,... | collective-permute-start | bytes 1572872 | tf_op jit(solution)/shard_map/ppermute | solution.py:25
  7.2 22.9 %collective-permute-start = (bf16[128,2048]{1,0:T(8,128)(2,1)}, bf16[128,2048]{1,0:T(8,128)(2,1)S(1)}, u32[]{:S(2)}, u32[]{:S(2)}) collective-permute-start(bf16[128,2048]{1,0:T(8,128)(2,1)} %get-tuple-element.12), channel_id=1, source_target_pairs={{0,1},{1,0},{2,3},{3,2},{4,6},{5,7},{6,4},{7,5},{8,9},{9,8},{10,11... | collective-permute-start | bytes 1572872 | tf_op jit(solution)/shard_map/ppermute | solution.py:25
  9.1 32.3 %collective-permute-start.9 = (bf16[256,1024]{1,0:T(8,128)(2,1)}, bf16[256,1024]{1,0:T(8,128)(2,1)}, u32[]{:S(2)}, u32[]{:S(2)}) collective-permute-start(bf16[256,1024]{1,0:T(8,128)(2,1)} %dynamic_slice.25), channel_id=1, source_target_pairs={{0,1},{1,0},{2,3},{3,2},{4,6},{5,7},{6,4},{7,5},{8,9},{9,8},{10,11... | collective-permute-start | bytes 1572872 | tf_op jit(solution)/shard_map/ppermute | solution.py:25
  11.1 8.7 %copy-start.1 = (bf16[2048,1024]{1,0:T(8,128)(2,1)S(1)}, bf16[2048,1024]{1,0:T(8,128)(2,1)}, u32[]{:S(2)}) copy-start(bf16[2048,1024]{1,0:T(8,128)(2,1)} %param.5) | copy-start | bytes 12582916
  14.9 8.7 %copy-start = (bf16[2048,1024]{1,0:T(8,128)(2,1)S(1)}, bf16[2048,1024]{1,0:T(8,128)(2,1)}, u32[]{:S(2)}) copy-start(bf16[2048,1024]{1,0:T(8,128)(2,1)} %param.6) | copy-start | bytes 12582916
  21.6 22.5 %collective-permute-start.4 = (bf16[128,1024]{1,0:T(8,128)(2,1)S(1)}, bf16[128,1024]{1,0:T(8,128)(2,1)S(1)}, u32[]{:S(2)}, u32[]{:S(2)}) collective-permute-start(bf16[128,1024]{1,0:T(8,128)(2,1)S(1)} %convolution_convert_fusion.7), channel_id=1, source_target_pairs={{0,1},{1,0},{2,3},{3,2},{4,6},{5,7},{6,4},{7,5},{8,9},{9,8},{10,11... | collective-permute-start | bytes 786440 | tf_op jit(solution)/shard_map/ppermute | solution.py:25
  25.4 22.9 %collective-permute-start.7 = (bf16[128,1024]{1,0:T(8,128)(2,1)S(1)}, bf16[128,1024]{1,0:T(8,128)(2,1)S(1)}, u32[]{:S(2)}, u32[]{:S(2)}) collective-permute-start(bf16[128,1024]{1,0:T(8,128)(2,1)S(1)} %convolution_convert_fusion.5), channel_id=1, source_target_pairs={{0,2},{1,3},{2,0},{3,1},{4,5},{5,4},{6,7},{7,6},{8,10},{9,11},{10,... | collective-permute-start | bytes 786440 | tf_op jit(solution)/shard_map/ppermute | solution.py:25
  30.9 19.7 %collective-permute-start.1 = (bf16[128,1024]{1,0:T(8,128)(2,1)S(1)}, bf16[128,1024]{1,0:T(8,128)(2,1)S(1)}, u32[]{:S(2)}, u32[]{:S(2)}) collective-permute-start(bf16[128,1024]{1,0:T(8,128)(2,1)S(1)} %convolution_convert_fusion.8), channel_id=1, source_target_pairs={{0,1},{1,0},{2,3},{3,2},{4,6},{5,7},{6,4},{7,5},{8,9},{9,8},{10,11... | collective-permute-start | bytes 786440 | tf_op jit(solution)/shard_map/ppermute | solution.py:25
  34.1 19.7 %collective-permute-start.6 = (bf16[128,1024]{1,0:T(8,128)(2,1)}, bf16[128,1024]{1,0:T(8,128)(2,1)}, u32[]{:S(2)}, u32[]{:S(2)}) collective-permute-start(bf16[128,1024]{1,0:T(8,128)(2,1)} %convolution_convert_fusion.6), channel_id=1, source_target_pairs={{0,2},{1,3},{2,0},{3,1},{4,5},{5,4},{6,7},{7,6},{8,10},{9,11},{10,... | collective-permute-start | bytes 786440 | tf_op jit(solution)/shard_map/ppermute | solution.py:25
  41.3 20.4 %collective-permute-start.10 = (bf16[256,1024]{1,0:T(8,128)(2,1)}, bf16[256,1024]{1,0:T(8,128)(2,1)}, u32[]{:S(2)}, u32[]{:S(2)}) collective-permute-start(bf16[256,1024]{1,0:T(8,128)(2,1)} %collective-permute-done.9), channel_id=1, source_target_pairs={{0,8},{4,12},{8,0},{12,4},{16,24},{20,28},{24,16},{28,20},{1,9},{5... | collective-permute-start | bytes 1572872 | tf_op jit(solution)/shard_map/ppermute | solution.py:29
  44.1 27.3 %collective-permute-start.11 = (bf16[256,1024]{1,0:T(8,128)(2,1)}, bf16[256,1024]{1,0:T(8,128)(2,1)}, u32[]{:S(2)}, u32[]{:S(2)}) collective-permute-start(bf16[256,1024]{1,0:T(8,128)(2,1)} %collective-permute-done.9), channel_id=1, source_target_pairs={{0,16},{4,20},{8,24},{12,28},{16,0},{20,4},{24,8},{28,12},{1,17},{... | collective-permute-start | bytes 1572872 | tf_op jit(solution)/shard_map/ppermute | solution.py:29
  48.3 9.2 %collective-permute-start.5 = (bf16[128,1024]{1,0:T(8,128)(2,1)}, bf16[128,1024]{1,0:T(8,128)(2,1)S(1)}, u32[]{:S(2)}, u32[]{:S(2)}) collective-permute-start(bf16[128,1024]{1,0:T(8,128)(2,1)} %fusion.13), channel_id=1, source_target_pairs={{0,2},{1,3},{2,0},{3,1},{4,5},{5,4},{6,7},{7,6},{8,10},{9,11},{10,... | collective-permute-start | bytes 786440 | tf_op jit(solution)/shard_map/ppermute | solution.py:25
  50.6 7.6 %collective-permute-start.8 = (bf16[128,1024]{1,0:T(8,128)(2,1)S(1)}, bf16[128,1024]{1,0:T(8,128)(2,1)}, u32[]{:S(2)}, u32[]{:S(2)}) collective-permute-start(bf16[128,1024]{1,0:T(8,128)(2,1)S(1)} %fusion.14), channel_id=1, source_target_pairs={{0,1},{1,0},{2,3},{3,2},{4,6},{5,7},{6,4},{7,5},{8,9},{9,8},{10,11... | collective-permute-start | bytes 786440 | tf_op jit(solution)/shard_map/ppermute | solution.py:25
  52.2 6.0 %copy-start.5 = (f32[128,1024]{1,0:T(8,128)S(1)}, f32[128,1024]{1,0:T(8,128)}, u32[]{:S(2)}) copy-start(f32[128,1024]{1,0:T(8,128)} %fusion.15) | copy-start | bytes 1572868
  53.8 17.8 %copy-start.2 = (bf16[1024,2048]{1,0:T(8,128)(2,1)S(1)}, bf16[1024,2048]{1,0:T(8,128)(2,1)}, u32[]{:S(2)}) copy-start(bf16[1024,2048]{1,0:T(8,128)(2,1)} %param.7) | copy-start | bytes 12582916
  53.8 20.7 %collective-permute-start.14 = (bf16[256,1024]{1,0:T(8,128)(2,1)}, bf16[256,1024]{1,0:T(8,128)(2,1)S(1)}, u32[]{:S(2)}, u32[]{:S(2)}) collective-permute-start(bf16[256,1024]{1,0:T(8,128)(2,1)} %collective-permute-done.9), channel_id=1, source_target_pairs={{0,4},{4,0},{8,12},{12,8},{16,20},{20,16},{24,28},{28,24},{1,5},{5... | collective-permute-start | bytes 1572872 | tf_op jit(solution)/shard_map/ppermute | solution.py:29
  57.5 21.8 %collective-permute-start.13 = (bf16[256,1024]{1,0:T(8,128)(2,1)}, bf16[256,1024]{1,0:T(8,128)(2,1)S(1)}, u32[]{:S(2)}, u32[]{:S(2)}) collective-permute-start(bf16[256,1024]{1,0:T(8,128)(2,1)} %collective-permute-done.9), channel_id=1, source_target_pairs={{8,16},{12,20},{16,8},{20,12},{9,17},{13,21},{17,9},{21,13},{10,18... | collective-permute-start | bytes 1572872 | tf_op jit(solution)/shard_map/ppermute | solution.py:29
  59.5 17.6 %collective-permute-start.20 = (bf16[128,1024]{1,0:T(8,128)(2,1)S(1)}, bf16[128,1024]{1,0:T(8,128)(2,1)S(1)}, u32[]{:S(2)}, u32[]{:S(2)}) collective-permute-start(bf16[128,1024]{1,0:T(8,128)(2,1)S(1)} %multiply_convert_fusion), channel_id=1, source_target_pairs={{0,1},{1,0},{2,3},{3,2},{4,6},{5,7},{6,4},{7,5},{8,9},{9,8},{10,11... | collective-permute-start | bytes 786440 | tf_op jit(solution)/shard_map/ppermute | solution.py:25
  61.7 14.4 %collective-permute-start.18 = (bf16[128,1024]{1,0:T(8,128)(2,1)S(1)}, bf16[128,1024]{1,0:T(8,128)(2,1)S(1)}, u32[]{:S(2)}, u32[]{:S(2)}) collective-permute-start(bf16[128,1024]{1,0:T(8,128)(2,1)S(1)} %multiply_convert_fusion), channel_id=1, source_target_pairs={{0,2},{1,3},{2,0},{3,1},{4,5},{5,4},{6,7},{7,6},{8,10},{9,11},{10,... | collective-permute-start | bytes 786440 | tf_op jit(solution)/shard_map/ppermute | solution.py:25
  71.3 20.2 %collective-permute-start.15 = (bf16[256,1024]{1,0:T(8,128)(2,1)}, bf16[256,1024]{1,0:T(8,128)(2,1)S(1)}, u32[]{:S(2)}, u32[]{:S(2)}) collective-permute-start(bf16[256,1024]{1,0:T(8,128)(2,1)} %collective-permute-done.10), channel_id=1, source_target_pairs={{0,4},{4,0},{8,12},{12,8},{16,20},{20,16},{24,28},{28,24},{1,5},{5... | collective-permute-start | bytes 1572872 | tf_op jit(solution)/shard_map/ppermute | solution.py:29
  74.5 16.4 %collective-permute-start.12 = (bf16[256,1024]{1,0:T(8,128)(2,1)}, bf16[256,1024]{1,0:T(8,128)(2,1)S(1)}, u32[]{:S(2)}, u32[]{:S(2)}) collective-permute-start(bf16[256,1024]{1,0:T(8,128)(2,1)} %collective-permute-done.11), channel_id=1, source_target_pairs={{16,24},{20,28},{8,0},{12,4},{17,25},{21,29},{9,1},{13,5},{18,26},... | collective-permute-start | bytes 1572872 | tf_op jit(solution)/shard_map/ppermute | solution.py:29
  76.1 17.3 %collective-permute-start.16 = (bf16[256,1024]{1,0:T(8,128)(2,1)}, bf16[256,1024]{1,0:T(8,128)(2,1)S(1)}, u32[]{:S(2)}, u32[]{:S(2)}) collective-permute-start(bf16[256,1024]{1,0:T(8,128)(2,1)} %collective-permute-done.11), channel_id=1, source_target_pairs={{0,4},{4,0},{8,12},{12,8},{16,20},{20,16},{24,28},{28,24},{1,5},{5... | collective-permute-start | bytes 1572872 | tf_op jit(solution)/shard_map/ppermute | solution.py:29
  77.1 18.5 %collective-permute-start.19 = (bf16[128,1024]{1,0:T(8,128)(2,1)S(1)}, bf16[128,1024]{1,0:T(8,128)(2,1)S(1)}, u32[]{:S(2)}, u32[]{:S(2)}) collective-permute-start(bf16[128,1024]{1,0:T(8,128)(2,1)S(1)} %fusion.5), channel_id=1, source_target_pairs={{0,2},{1,3},{2,0},{3,1},{4,5},{5,4},{6,7},{7,6},{8,10},{9,11},{10,... | collective-permute-start | bytes 786440 | tf_op jit(solution)/shard_map/ppermute | solution.py:25
  79.4 16.4 %collective-permute-start.21 = (bf16[128,1024]{1,0:T(8,128)(2,1)S(1)}, bf16[128,1024]{1,0:T(8,128)(2,1)S(1)}, u32[]{:S(2)}, u32[]{:S(2)}) collective-permute-start(bf16[128,1024]{1,0:T(8,128)(2,1)S(1)} %fusion.8), channel_id=1, source_target_pairs={{0,1},{1,0},{2,3},{3,2},{4,6},{5,7},{6,4},{7,5},{8,9},{9,8},{10,11... | collective-permute-start | bytes 786440 | tf_op jit(solution)/shard_map/ppermute | solution.py:25
  91.0 2.9 %collective-permute-start.17 = (bf16[256,1024]{1,0:T(8,128)(2,1)S(1)}, bf16[256,1024]{1,0:T(8,128)(2,1)S(1)}, u32[]{:S(2)}, u32[]{:S(2)}) collective-permute-start(bf16[256,1024]{1,0:T(8,128)(2,1)S(1)} %broadcast_select_fusion), channel_id=1, source_target_pairs={{0,4},{4,0},{8,12},{12,8},{16,20},{20,16},{24,28},{28,24},{1,5},{5... | collective-permute-start | bytes 1572872 | tf_op jit(solution)/shard_map/ppermute | solution.py:29
  91.6 7.4 %collective-permute-start.22 = (bf16[128,1024]{1,0:T(8,128)(2,1)S(1)}, bf16[128,1024]{1,0:T(8,128)(2,1)S(1)}, u32[]{:S(2)}, u32[]{:S(2)}) collective-permute-start(bf16[128,1024]{1,0:T(8,128)(2,1)S(1)} %convolution_convert_fusion.2), channel_id=1, source_target_pairs={{0,2},{1,3},{2,0},{3,1},{4,5},{5,4},{6,7},{7,6},{8,10},{9,11},{10,... | collective-permute-start | bytes 786440 | tf_op jit(solution)/shard_map/ppermute | solution.py:25
  94.4 6.4 %collective-permute-start.23 = (bf16[128,1024]{1,0:T(8,128)(2,1)S(1)}, bf16[128,1024]{1,0:T(8,128)(2,1)S(1)}, u32[]{:S(2)}, u32[]{:S(2)}) collective-permute-start(bf16[128,1024]{1,0:T(8,128)(2,1)S(1)} %convolution_convert_fusion.1), channel_id=1, source_target_pairs={{0,1},{1,0},{2,3},{3,2},{4,6},{5,7},{6,4},{7,5},{8,9},{9,8},{10,11... | collective-permute-start | bytes 786440 | tf_op jit(solution)/shard_map/ppermute | solution.py:25
  99.0 1.9 %copy-start.4 = (bf16[128,8192]{1,0:T(8,128)(2,1)}, bf16[128,8192]{1,0:T(8,128)(2,1)S(1)}, u32[]{:S(2)}) copy-start(bf16[128,8192]{1,0:T(8,128)(2,1)S(1)} %constant_dynamic-update-slice_fusion.1) | copy-start | bytes 6291460
where the time goes:
time: 102 us
  waiting for transfers between devices  43 us (42%)
  starting transfers between devices  31 us (30%)
  matrix products  16 us (16%)
  local copies, waits for them, and re-layouts  9.57 us (9%)
  other arithmetic  1.38 us (1%)
    ppermute x16, starting transfers between devices, send(): return lax.ppermute(x, ('dp', 'row', 'col'), pairs)  23.8 us
    ppermute x16, waiting for transfers between devices, send(): return lax.ppermute(x, ('dp', 'row', 'col'), pairs)  23.4 us
    ppermute x8, waiting for transfers between devices, send_dp(): return lax.ppermute(x, 'dp', pairs)  19.6 us
    dot_general x15, matrix products, matmul(): return jnp.dot(x, y, preferred_element_type=jnp.float32)  16 us
    ppermute x8, starting transfers between devices, send_dp(): return lax.ppermute(x, 'dp', pairs)  7.25 us
    dynamic_update_slice x8, local copies, waits for them, and re-layouts, fill(): lax.dynamic_update_slice_in_dim(far[i], rows_of, from_chip * share, axis=0)  3.47 us
    dynamic_slice x1, local copies, waits for them, and re-layouts, columns(): return lax.dynamic_slice_in_dim(x, at, size, axis=1)  2.71 us
  transfers between devices with their start and end apart: 24, of which 10 were waited for; matrix products, arithmetic and copies ran while one was open for 23% of the time, Pallas kernels for 0%

commit v1 on v0

v1 whole, which is shorter than its diff:
```python
import jax
import jax.numpy as jnp
from jax import lax
from jax.sharding import PartitionSpec as P


def solution(mesh):
    rows, cols, dp = mesh.shape["row"], mesh.shape["col"], mesh.shape["dp"]
    cores = 2 if dp % 2 == 0 else 1
    chips = dp // cores
    turned = cores == 2 and rows == cols
    line = turned and chips == 4
    shifts = [(dr, dc) for dr in range(rows) for dc in range(cols)]
    away = [s for s in shifts if s != (0, 0)]

    def send(x, shift):
        dr, dc = shift
        pairs = [
            (r * cols + c, (r + dr) % rows * cols + (c + dc) % cols) for r in range(rows) for c in range(cols)
        ]
        return lax.ppermute(x, ("row", "col"), pairs)

    def send_turned(x, shift):
        pairs = []
        for d in range(dp):
            dr, dc = shift if turned and d % cores else shift[::-1]
            for r in range(rows):
                for c in range(cols):
                    to = (d * rows + (r + dr) % rows) * cols + (c + dc) % cols
                    pairs.append(((d * rows + r) * cols + c, to))
        return lax.ppermute(x, ("dp", "row", "col"), pairs)

    def send_dp(x, chip_pairs, core_shift):
        pairs = [(z * cores + k, to * cores + (k + core_shift) % cores) for z, to in chip_pairs for k in range(cores)]
        return lax.ppermute(x, "dp", pairs)

    def matmul(x, y):
        return jnp.dot(x, y, preferred_element_type=jnp.float32)

    def shards(tokens, w_gate, w_up, w_down):
        r, c, d = lax.axis_index("row"), lax.axis_index("col"), lax.axis_index("dp")
        chip, core = d // cores, d % cores
        slab = w_gate.shape[0]
        hidden_width, width = w_down.shape
        half = width // 2
        at_b = core * half if turned else 0
        at_a = half - at_b

        def place(dr, dc):
            return (r + dr) % rows * cols + (c + dc) % cols

        def place_turned(a, b):
            return place(b + core * (a - b), a + core * (b - a)) if turned else place(b, a)

        def columns(x, at, size):
            return lax.dynamic_slice_in_dim(x, at, size, axis=1)

        early, late = [], []
        if turned:
            share = hidden_width // dp
            block = (rows - 1) * share
            piece = lax.dynamic_slice_in_dim(w_down, d * share, share, axis=0)
            along_col = [send(piece[:, :half], (0, -dc)) for dc in range(1, cols)]
            along_row = [send(piece[:, half:], (-dr, 0)) for dr in range(1, rows)]
            held = jnp.zeros((2 * block, half), jnp.bfloat16)
            for i in range(rows - 1):
                held = lax.dynamic_update_slice_in_dim(held, along_col[i], core * block + i * share, axis=0)
                held = lax.dynamic_update_slice_in_dim(held, along_row[i], (1 - core) * block + i * share, axis=0)

        feats = {s: columns(tokens, place(*s) * slab, slab) for s in shifts}
        got = {s: send(feats[s], s) for s in away}
        got[0, 0] = feats[0, 0]

        if line:
            two = send_dp(held, [(z, z ^ 2) for z in range(chips)], 0)
            one = send_dp(held, [(z, z ^ 1) for z in range(chips)], 0)
            middle = send_dp(held, [(1, 2), (2, 1)], 0)
            early += [(one, chip ^ 1), (two, chip ^ 2)]
        elif turned:
            for z in range(1, chips):
                turn = send_dp(held, [(i, (i + z) % chips) for i in range(chips)], 0)
                late.append((turn, (chip - z) % chips))

        def crossed(weight, col_first):
            first, second = (cols, rows) if col_first else (rows, cols)

            def shift(i, j):
                return (j, i) if col_first else (i, j)

            parts = {s: matmul(got[s], weight) for s in away}
            parts[0, 0] = matmul(got[0, 0], weight)
            sums = {j: parts[shift(0, j)] for j in range(second)}
            for j in reversed(range(second)):
                for i in range(1, first):
                    part = send(parts[shift(i, j)].astype(jnp.bfloat16), shift(-i, 0))
                    sums[j] = sums[j] + part.astype(jnp.float32)
            total = sums[0]
            passed = [sums[j].astype(jnp.bfloat16) for j in range(1, second)]
            for j in range(1, second):
                total = total + send(passed[j - 1], shift(0, -j)).astype(jnp.float32)
            return total, passed

        gate, gate_passed = crossed(w_gate, True)
        up, up_passed = crossed(w_up, False)
        hidden = (jax.nn.silu(gate) * up).astype(jnp.bfloat16)

        if turned:
            if line:
                relayed = send_dp(two, [(2, 3), (1, 0)], 0)
                late.append((jnp.where((chip == 0) | (chip == chips - 1), relayed, middle), chip ^ 3))
            far_b = {a: jnp.zeros((hidden_width, half), jnp.bfloat16) for a in range(1, rows)}
            far_a = {b: jnp.zeros((hidden_width, half), jnp.bfloat16) for b in range(1, rows)}

            def fill(pieces):
                for k in range(cores):
                    for moved, from_chip in pieces:
                        if k:
                            moved = send_dp(moved, [(z, z) for z in range(chips)], k)
                        at = (from_chip * cores + core + k * (1 - 2 * core)) * share
                        for i, far in enumerate([far_a, far_b] if k else [far_b, far_a]):
                            for j in range(1, rows):
                                lower = i * block + (j - 1) * share
                                far[j] = lax.dynamic_update_slice_in_dim(far[j], moved[lower : lower + share], at, axis=0)

            fill([(held, chip)])
            tied, _ = lax.optimization_barrier(([p for p, _ in early], gate_passed + up_passed))
            fill([(p, at) for p, (_, at) in zip(tied, early)])
        else:
            far_b = {a: send(w_down[:, :half], (0, -a)) for a in range(1, cols)}
            far_a = {b: send(w_down[:, half:], (-b, 0)) for b in range(1, rows)}

        near_b = {b: send_turned(hidden, (0, -b)) for b in far_a}
        near_a = {a: send_turned(hidden, (-a, 0)) for a in far_b}
        w_b, w_a = columns(w_down, at_b, half), columns(w_down, at_a, half)

        outs = []

        def give(x, weight, shift, slab_from, at):
            out = send_turned(matmul(x, weight).astype(jnp.bfloat16), shift)
            outs.append((out, place_turned(*slab_from) * width + at))

        for b, other in near_b.items():
            give(other, w_b, (0, b), (0, -b), at_b)
        for a, other in near_a.items():
            give(other, w_a, (a, 0), (-a, 0), at_a)
        if turned:
            tied, _ = lax.optimization_barrier(([p for p, _ in late], hidden))
            fill([(p, at) for p, (_, at) in zip(tied, late)])
        for b, other in near_b.items():
            for a in far_b:
                give(other, far_b[a], (0, b), (a, -b), at_b)
        for a, other in near_a.items():
            for b in far_a:
                give(other, far_a[b], (a, 0), (-a, b), at_a)

        def keep(weight):
            return matmul(hidden, weight).astype(jnp.bfloat16)

        landed = [(keep(w_down), place(0, 0) * width)]
        for a in far_b:
            landed.append((keep(far_b[a]), place_turned(a, 0) * width + at_b))
        for b in far_a:
            landed.append((keep(far_a[b]), place_turned(0, b) * width + at_a))
        mixed = jnp.zeros((tokens.shape[0], width * rows * cols), jnp.bfloat16)
        for block, at in landed + outs:
            mixed = lax.dynamic_update_slice_in_dim(mixed, block, at, axis=1)
        return mixed

    in_specs = (
        P(("dp", "row", "col"), None),
        P(("row", "col"), None),
        P(("row", "col"), None),
        P(None, ("row", "col")),
    )
    out_specs = P(("dp", "row", "col"), None)
    return jax.shard_map(shards, mesh=mesh, in_specs=in_specs, out_specs=out_specs, check_vma=False)
```

time: 102 us -> 94.7 us (0.928)
  starting transfers between devices: 31 us -> 26.7 us
  other arithmetic: 1.38 us -> 0.36 us
    ppermute x8, waiting for transfers between devices: 19.6 us -> 9.18 us  [send_dp(): return lax.ppermute(x, 'dp', pairs)]
    ppermute x16 -> x17, waiting for transfers between devices: 23.4 us -> 33.4 us  [the longest x11 25.9 us: send(): return lax.ppermute(x, ('row', 'col'), pairs)]
    ppermute x16 -> x17, starting transfers between devices: 23.8 us -> 20.4 us  [the longest x11 13.9 us: send(): return lax.ppermute(x, ('row', 'col'), pairs)]
    slice x0 -> x1, local copies, waits for them, and re-layouts: none -> 1.92 us  [shards(): along_row = [send(piece[:, half:], (-dr, 0)) for dr in range(1, rows)]]
    dynamic_slice x1 -> x0, local copies, waits for them, and re-layouts: 1.87 us -> none  [shards(): piece = lax.dynamic_slice(w_down, (chip * share, at_b), (share, half))]
    dynamic_update_slice x8 -> x11, local copies, waits for them, and re-layouts: 3.47 us -> 2.34 us  [the longest x1 0.97 us: shards(): lax.dynamic_update_slice_in_dim(held, along_col[i], core * block + i * sh...]
  transfers between devices with their start and end apart: 24 -> 25, of which waited for: 10 -> 12; matrix products, arithmetic and copies ran while one was open for 23% -> 23% of each run, Pallas kernels for 0% -> 0%
where the time goes in v1:
time: 94.7 us; the launch traced here: 94.2 us
  waiting for transfers between devices  42.6 us (45%)
  starting transfers between devices  26.7 us (28%)
  matrix products  15.4 us (16%)
  local copies, waits for them, and re-layouts  8.73 us (9%)
    ppermute x11, waiting for transfers between devices, send(): return lax.ppermute(x, ('row', 'col'), pairs)  25.9 us
    dot_general x15, matrix products, matmul(): return jnp.dot(x, y, preferred_element_type=jnp.float32)  15.4 us
    ppermute x11, starting transfers between devices, send(): return lax.ppermute(x, ('row', 'col'), pairs)  13.9 us
    ppermute x8, waiting for transfers between devices, send_dp(): return lax.ppermute(x, 'dp', pairs)  9.18 us
    ppermute x6, waiting for transfers between devices, send_turned(): return lax.ppermute(x, ('dp', 'row', 'col'), pairs)  7.44 us
    ppermute x6, starting transfers between devices, send_turned(): return lax.ppermute(x, ('dp', 'row', 'col'), pairs)  6.47 us
    ppermute x8, starting transfers between devices, send_dp(): return lax.ppermute(x, 'dp', pairs)  6.33 us
    dynamic_slice x1, local copies, waits for them, and re-layouts, columns(): return lax.dynamic_slice_in_dim(x, at, size, axis=1)  2.57 us
  transfers between devices with their start and end apart: 25, of which 12 were waited for; matrix products, arithmetic and copies ran while one was open for 23% of the time, Pallas kernels for 0%

profile of v1, /device:TPU:0, one launch (start us, length us, event | category | flops | bytes accessed | tf_op | source)
XLA Modules:
  0.0 94.2 jit_solution(3029594953606210750)
XLA Ops:
  0.0 1.9 %fusion.23 = (bf16[128,1024]{1,0:T(8,128)(2,1)S(1)}, bf16[128,1024]{1,0:T(8,128)(2,1)}) fusion(bf16[1024,2048]{1,0:T(8,128)(2,1)} %param.7, s32[]{:T(128)S(6)} %select_n.181, s32[]{:T(128)S(6)} %add.386), kind=kLoop, calls=%fused_computation.58 | loop fusion | bytes 1048584 | tf_op jit(solution)/shard_map/slice | solution.py:64
  1.9 3.0 %collective-permute-start.9 = (bf16[128,1024]{1,0:T(8,128)(2,1)}, bf16[128,1024]{1,0:T(8,128)(2,1)}, u32[]{:S(2)}, u32[]{:S(2)}) collective-permute-start(bf16[128,1024]{1,0:T(8,128)(2,1)} %get-tuple-element.12), channel_id=1, source_target_pairs={{0,1},{1,0},{2,3},{3,2},{4,5},{5,4},{6,7},{7,6},{8,9},{9,8},{10,11... | collective-permute-start | bytes 786440 | tf_op jit(solution)/shard_map/ppermute | solution.py:21
  4.9 1.5 %collective-permute-start.10 = (bf16[128,1024]{1,0:T(8,128)(2,1)S(1)}, bf16[128,1024]{1,0:T(8,128)(2,1)}, u32[]{:S(2)}, u32[]{:S(2)}) collective-permute-start(bf16[128,1024]{1,0:T(8,128)(2,1)S(1)} %get-tuple-element.11), channel_id=1, source_target_pairs={{0,2},{1,3},{2,0},{3,1},{4,6},{5,7},{6,4},{7,5},{8,10},{9,11},{10,... | collective-permute-start | bytes 786440 | tf_op jit(solution)/shard_map/ppermute | solution.py:21
  6.4 2.6 %constant_dynamic-slice_fusion.2 = (bf16[128,2048]{1,0:T(8,128)(2,1)}, bf16[128,2048]{1,0:T(8,128)(2,1)}, bf16[128,2048]{1,0:T(8,128)(2,1)}) fusion(bf16[128,8192]{1,0:T(8,128)(2,1)} %param.4, s32[]{:T(128)S(6)} %select_n.179, s32[]{:T(128)S(6)} %select_n.177, s32[]{:T(128)S(6)} %select_n.180), kind=kLoop, calls=%fused_computation.55 | loop fusion | bytes 3145740 | tf_op jit(solution)/shard_map/dynamic_slice | solution.py:56
  9.0 2.0 %collective-permute-start.2 = (bf16[128,2048]{1,0:T(8,128)(2,1)}, bf16[128,2048]{1,0:T(8,128)(2,1)S(1)}, u32[]{:S(2)}, u32[]{:S(2)}) collective-permute-start(bf16[128,2048]{1,0:T(8,128)(2,1)} %get-tuple-element.13), channel_id=1, source_target_pairs={{0,2},{1,3},{2,0},{3,1},{4,6},{5,7},{6,4},{7,5},{8,10},{9,11},{10,... | collective-permute-start | bytes 1572872 | tf_op jit(solution)/shard_map/ppermute | solution.py:21
  10.9 1.5 %collective-permute-start = (bf16[128,2048]{1,0:T(8,128)(2,1)}, bf16[128,2048]{1,0:T(8,128)(2,1)S(1)}, u32[]{:S(2)}, u32[]{:S(2)}) collective-permute-start(bf16[128,2048]{1,0:T(8,128)(2,1)} %get-tuple-element.14), channel_id=1, source_target_pairs={{0,1},{1,0},{2,3},{3,2},{4,5},{5,4},{6,7},{7,6},{8,9},{9,8},{10,11... | collective-permute-start | bytes 1572872 | tf_op jit(solution)/shard_map/ppermute | solution.py:21
  12.5 3.8 %fusion.15 = f32[128,1024]{1,0:T(8,128)} fusion(bf16[2048,1024]{1,0:T(8,128)(2,1)} %param.6, bf16[128,8192]{1,0:T(8,128)(2,1)S(1)} %copy-done.4, s32[]{:T(128)S(6)} %select_n.175), kind=kOutput, calls=%fused_computation.24 | convolution fusion | flops 536870912 | bytes 5242884 | tf_op jit(solution)/shard_map/dot_general | solution.py:38
  16.3 1.6 %fusion.17 = f32[128,1024]{1,0:T(8,128)} fusion(bf16[2048,1024]{1,0:T(8,128)(2,1)S(1)} %copy-done, bf16[128,8192]{1,0:T(8,128)(2,1)S(1)} %copy-done.4, s32[]{:T(128)S(6)} %select_n.175), kind=kOutput, calls=%fused_computation.26 | convolution fusion | flops 536870912 | bytes 5242884 | tf_op jit(solution)/shard_map/dot_general | solution.py:38
  17.9 1.0 %constant_dynamic-update-slice_fusion.5 = bf16[256,1024]{1,0:T(8,128)(2,1)S(1)} fusion(bf16[256,1024]{1,0:T(8,128)(2,1)S(1)} %broadcast_in_dim.7, bf16[128,1024]{1,0:T(8,128)(2,1)} %collective-permute-done.9, s32[]{:T(128)S(6)} %select_n.183), kind=kLoop, calls=%fused_computation.53 | loop fusion | bytes 524292 | tf_op jit(solution)/shard_map/dynamic_update_slice | solution.py:67
  18.9 1.0 %constant_dynamic-update-slice_fusion.4 = bf16[256,1024]{1,0:T(8,128)(2,1)S(1)} fusion(bf16[256,1024]{1,0:T(8,128)(2,1)S(1)} %constant_dynamic-update-slice_fusion.5, bf16[128,1024]{1,0:T(8,128)(2,1)} %collective-permute-done.10, s32[]{:T(128)S(6)} %select_n.184), kind=kLoop, calls=%fused_computation.52 | loop fusion | bytes 524292 | tf_op jit(solution)/shard_map/dynamic_update_slice | solution.py:68
  20.0 1.6 %collective-permute-start.12 = (bf16[256,1024]{1,0:T(8,128)(2,1)S(1)}, bf16[256,1024]{1,0:T(8,128)(2,1)S(1)}, u32[]{:S(2)}, u32[]{:S(2)}) collective-permute-start(bf16[256,1024]{1,0:T(8,128)(2,1)S(1)} %constant_dynamic-update-slice_fusion.4), channel_id=1, source_target_pairs={{0,8},{4,12},{8,0},{12,4},{16,24},{20,28},{24,16},{28,20},{1,9},{5... | collective-permute-start | bytes 1572872 | tf_op jit(solution)/shard_map/ppermute | solution.py:35
  22.2 2.8 %collective-permute-done.3 = bf16[128,2048]{1,0:T(8,128)(2,1)} collective-permute-done((bf16[128,2048]{1,0:T(8,128)(2,1)}, bf16[128,2048]{1,0:T(8,128)(2,1)}, u32[]{:S(2)}, u32[]{:S(2)}) %collective-permute-start.3) | collective-permute-done | bytes 524320 | tf_op jit(solution)/shard_map/ppermute | solution.py:21
  25.0 2.6 %collective-permute-start.13 = (bf16[256,1024]{1,0:T(8,128)(2,1)S(1)}, bf16[256,1024]{1,0:T(8,128)(2,1)S(1)}, u32[]{:S(2)}, u32[]{:S(2)}) collective-permute-start(bf16[256,1024]{1,0:T(8,128)(2,1)S(1)} %constant_dynamic-update-slice_fusion.4), channel_id=1, source_target_pairs={{0,16},{4,20},{8,24},{12,28},{16,0},{20,4},{24,8},{28,12},{1,17},{... | collective-permute-start | bytes 1572872 | tf_op jit(solution)/shard_map/ppermute | solution.py:35
  27.6 1.8 %convolution_convert_fusion.7 = bf16[128,1024]{1,0:T(8,128)(2,1)S(1)} fusion(bf16[128,2048]{1,0:T(8,128)(2,1)} %collective-permute-done.3, bf16[2048,1024]{1,0:T(8,128)(2,1)S(1)} %copy-done.1), kind=kOutput, calls=%fused_computation.20 | convolution fusion | flops 537001984 | bytes 4980736 | tf_op jit(solution)/shard_map/dot_general | solution.py:38
  29.4 1.8 %convolution_convert_fusion.5 = bf16[128,1024]{1,0:T(8,128)(2,1)S(1)} fusion(bf16[128,2048]{1,0:T(8,128)(2,1)} %collective-permute-done.3, bf16[2048,1024]{1,0:T(8,128)(2,1)S(1)} %copy-done.2), kind=kOutput, calls=%fused_computation.18 | convolution fusion | flops 537001984 | bytes 4980736 | tf_op jit(solution)/shard_map/dot_general | solution.py:38
  31.3 3.4 %collective-permute-done = bf16[128,2048]{1,0:T(8,128)(2,1)S(1)} collective-permute-done((bf16[128,2048]{1,0:T(8,128)(2,1)}, bf16[128,2048]{1,0:T(8,128)(2,1)S(1)}, u32[]{:S(2)}, u32[]{:S(2)}) %collective-permute-start) | collective-permute-done | bytes 524320 | tf_op jit(solution)/shard_map/ppermute | solution.py:21
  36.1 1.2 %collective-permute-start.4 = (bf16[128,1024]{1,0:T(8,128)(2,1)S(1)}, bf16[128,1024]{1,0:T(8,128)(2,1)S(1)}, u32[]{:S(2)}, u32[]{:S(2)}) collective-permute-start(bf16[128,1024]{1,0:T(8,128)(2,1)S(1)} %convolution_convert_fusion.7), channel_id=1, source_target_pairs={{0,1},{1,0},{2,3},{3,2},{4,5},{5,4},{6,7},{7,6},{8,9},{9,8},{10,11... | collective-permute-start | bytes 786440 | tf_op jit(solution)/shard_map/ppermute | solution.py:21
  38.1 6.1 %collective-permute-done.4 = bf16[128,1024]{1,0:T(8,128)(2,1)S(1)} collective-permute-done((bf16[128,1024]{1,0:T(8,128)(2,1)S(1)}, bf16[128,1024]{1,0:T(8,128)(2,1)S(1)}, u32[]{:S(2)}, u32[]{:S(2)}) %collective-permute-start.4) | collective-permute-done | bytes 262176 | tf_op jit(solution)/shard_map/ppermute | solution.py:21
  45.6 5.8 %collective-permute-done.7 = bf16[128,1024]{1,0:T(8,128)(2,1)S(1)} collective-permute-done((bf16[128,1024]{1,0:T(8,128)(2,1)S(1)}, bf16[128,1024]{1,0:T(8,128)(2,1)S(1)}, u32[]{:S(2)}, u32[]{:S(2)}) %collective-permute-start.7) | collective-permute-done | bytes 262176 | tf_op jit(solution)/shard_map/ppermute | solution.py:21
  52.2 1.4 %collective-permute-start.6 = (bf16[128,1024]{1,0:T(8,128)(2,1)S(1)}, bf16[128,1024]{1,0:T(8,128)(2,1)S(1)}, u32[]{:S(2)}, u32[]{:S(2)}) collective-permute-start(bf16[128,1024]{1,0:T(8,128)(2,1)S(1)} %convolution_convert_fusion.6), channel_id=1, source_target_pairs={{0,2},{1,3},{2,0},{3,1},{4,6},{5,7},{6,4},{7,5},{8,10},{9,11},{10,... | collective-permute-start | bytes 786440 | tf_op jit(solution)/shard_map/ppermute | solution.py:21
  54.3 2.0 %collective-permute-start.8 = (bf16[128,1024]{1,0:T(8,128)(2,1)S(1)}, bf16[128,1024]{1,0:T(8,128)(2,1)S(1)}, u32[]{:S(2)}, u32[]{:S(2)}) collective-permute-start(bf16[128,1024]{1,0:T(8,128)(2,1)S(1)} %fusion.14), channel_id=1, source_target_pairs={{0,1},{1,0},{2,3},{3,2},{4,5},{5,4},{6,7},{7,6},{8,9},{9,8},{10,11... | collective-permute-start | bytes 786440 | tf_op jit(solution)/shard_map/ppermute | solution.py:21
  56.5 4.0 %collective-permute-done.1 = bf16[128,1024]{1,0:T(8,128)(2,1)S(1)} collective-permute-done((bf16[128,1024]{1,0:T(8,128)(2,1)S(1)}, bf16[128,1024]{1,0:T(8,128)(2,1)S(1)}, u32[]{:S(2)}, u32[]{:S(2)}) %collective-permute-start.1) | collective-permute-done | bytes 262176 | tf_op jit(solution)/shard_map/ppermute | solution.py:21
  61.4 2.8 %collective-permute-done.5 = bf16[128,1024]{1,0:T(8,128)(2,1)S(1)} collective-permute-done((bf16[128,1024]{1,0:T(8,128)(2,1)S(1)}, bf16[128,1024]{1,0:T(8,128)(2,1)S(1)}, u32[]{:S(2)}, u32[]{:S(2)}) %collective-permute-start.5) | collective-permute-done | bytes 262176 | tf_op jit(solution)/shard_map/ppermute | solution.py:21
  64.2 1.3 %collective-permute-start.16 = (bf16[256,1024]{1,0:T(8,128)(2,1)S(1)}, bf16[256,1024]{1,0:T(8,128)(2,1)S(1)}, u32[]{:S(2)}, u32[]{:S(2)}) collective-permute-start(bf16[256,1024]{1,0:T(8,128)(2,1)S(1)} %collective-permute-done.13), channel_id=1, source_target_pairs={{16,24},{20,28},{8,0},{12,4},{17,25},{21,29},{9,1},{13,5},{18,26},... | collective-permute-start | bytes 1572872 | tf_op jit(solution)/shard_map/ppermute | solution.py:35
  67.4 1.6 %collective-permute-start.21 = (bf16[128,1024]{1,0:T(8,128)(2,1)S(1)}, bf16[128,1024]{1,0:T(8,128)(2,1)S(1)}, u32[]{:S(2)}, u32[]{:S(2)}) collective-permute-start(bf16[128,1024]{1,0:T(8,128)(2,1)S(1)} %multiply_convert_fusion), channel_id=1, source_target_pairs={{0,1},{1,0},{2,3},{3,2},{4,6},{5,7},{6,4},{7,5},{8,9},{9,8},{10,11... | collective-permute-start | bytes 786440 | tf_op jit(solution)/shard_map/ppermute | solution.py:31
  69.0 9.2 %collective-permute-done.16 = bf16[256,1024]{1,0:T(8,128)(2,1)S(1)} collective-permute-done((bf16[256,1024]{1,0:T(8,128)(2,1)S(1)}, bf16[256,1024]{1,0:T(8,128)(2,1)S(1)}, u32[]{:S(2)}, u32[]{:S(2)}) %collective-permute-start.16) | collective-permute-done | bytes 524320 | tf_op jit(solution)/shard_map/ppermute | solution.py:35
  78.8 1.0 %collective-permute-start.20 = (bf16[128,1024]{1,0:T(8,128)(2,1)S(1)}, bf16[128,1024]{1,0:T(8,128)(2,1)S(1)}, u32[]{:S(2)}, u32[]{:S(2)}) collective-permute-start(bf16[128,1024]{1,0:T(8,128)(2,1)S(1)} %fusion.5), channel_id=1, source_target_pairs={{0,2},{1,3},{2,0},{3,1},{4,5},{5,4},{6,7},{7,6},{8,10},{9,11},{10,... | collective-permute-start | bytes 786440 | tf_op jit(solution)/shard_map/ppermute | solution.py:31
  80.2 1.2 %collective-permute-start.22 = (bf16[128,1024]{1,0:T(8,128)(2,1)S(1)}, bf16[128,1024]{1,0:T(8,128)(2,1)S(1)}, u32[]{:S(2)}, u32[]{:S(2)}) collective-permute-start(bf16[128,1024]{1,0:T(8,128)(2,1)S(1)} %fusion.8), channel_id=1, source_target_pairs={{0,1},{1,0},{2,3},{3,2},{4,6},{5,7},{6,4},{7,5},{8,9},{9,8},{10,11... | collective-permute-start | bytes 786440 | tf_op jit(solution)/shard_map/ppermute | solution.py:31
  82.1 1.8 %collective-permute-start.23 = (bf16[128,1024]{1,0:T(8,128)(2,1)S(1)}, bf16[128,1024]{1,0:T(8,128)(2,1)S(1)}, u32[]{:S(2)}, u32[]{:S(2)}) collective-permute-start(bf16[128,1024]{1,0:T(8,128)(2,1)S(1)} %convolution_convert_fusion.2), channel_id=1, source_target_pairs={{0,2},{1,3},{2,0},{3,1},{4,5},{5,4},{6,7},{7,6},{8,10},{9,11},{10,... | collective-permute-start | bytes 786440 | tf_op jit(solution)/shard_map/ppermute | solution.py:31
  86.5 2.9 %collective-permute-done.22 = bf16[128,1024]{1,0:T(8,128)(2,1)S(1)} collective-permute-done((bf16[128,1024]{1,0:T(8,128)(2,1)S(1)}, bf16[128,1024]{1,0:T(8,128)(2,1)S(1)}, u32[]{:S(2)}, u32[]{:S(2)}) %collective-permute-start.22) | collective-permute-done | bytes 262176 | tf_op jit(solution)/shard_map/ppermute | solution.py:31
  89.5 2.7 %collective-permute-done.23 = bf16[128,1024]{1,0:T(8,128)(2,1)S(1)} collective-permute-done((bf16[128,1024]{1,0:T(8,128)(2,1)S(1)}, bf16[128,1024]{1,0:T(8,128)(2,1)S(1)}, u32[]{:S(2)}, u32[]{:S(2)}) %collective-permute-start.23) | collective-permute-done | bytes 262176 | tf_op jit(solution)/shard_map/ppermute | solution.py:31
  92.2 1.0 %collective-permute-done.24 = bf16[128,1024]{1,0:T(8,128)(2,1)S(1)} collective-permute-done((bf16[128,1024]{1,0:T(8,128)(2,1)S(1)}, bf16[128,1024]{1,0:T(8,128)(2,1)S(1)}, u32[]{:S(2)}, u32[]{:S(2)}) %collective-permute-start.24) | collective-permute-done | bytes 262176 | tf_op jit(solution)/shard_map/ppermute | solution.py:31
  (72 shorter events, 13.9 us)
Async XLA Ops:
  0.0 12.5 %copy-start.4 = (bf16[128,8192]{1,0:T(8,128)(2,1)S(1)}, bf16[128,8192]{1,0:T(8,128)(2,1)}, u32[]{:S(2)}) copy-start(bf16[128,8192]{1,0:T(8,128)(2,1)} %param.4) | copy-start | bytes 6291460
  1.9 16.0 %collective-permute-start.9 = (bf16[128,1024]{1,0:T(8,128)(2,1)}, bf16[128,1024]{1,0:T(8,128)(2,1)}, u32[]{:S(2)}, u32[]{:S(2)}) collective-permute-start(bf16[128,1024]{1,0:T(8,128)(2,1)} %get-tuple-element.12), channel_id=1, source_target_pairs={{0,1},{1,0},{2,3},{3,2},{4,5},{5,4},{6,7},{7,6},{8,9},{9,8},{10,11... | collective-permute-start | bytes 786440 | tf_op jit(solution)/shard_map/ppermute | solution.py:21
  4.9 14.0 %collective-permute-start.10 = (bf16[128,1024]{1,0:T(8,128)(2,1)S(1)}, bf16[128,1024]{1,0:T(8,128)(2,1)}, u32[]{:S(2)}, u32[]{:S(2)}) collective-permute-start(bf16[128,1024]{1,0:T(8,128)(2,1)S(1)} %get-tuple-element.11), channel_id=1, source_target_pairs={{0,2},{1,3},{2,0},{3,1},{4,6},{5,7},{6,4},{7,5},{8,10},{9,11},{10,... | collective-permute-start | bytes 786440 | tf_op jit(solution)/shard_map/ppermute | solution.py:21
  9.0 16.1 %collective-permute-start.3 = (bf16[128,2048]{1,0:T(8,128)(2,1)}, bf16[128,2048]{1,0:T(8,128)(2,1)}, u32[]{:S(2)}, u32[]{:S(2)}) collective-permute-start(bf16[128,2048]{1,0:T(8,128)(2,1)} %get-tuple-element.15), channel_id=1, source_target_pairs={{0,3},{1,2},{2,1},{3,0},{4,7},{5,6},{6,5},{7,4},{8,11},{9,10},{10,... | collective-permute-start | bytes 1572872 | tf_op jit(solution)/shard_map/ppermute | solution.py:21
  9.0 27.1 %collective-permute-start.2 = (bf16[128,2048]{1,0:T(8,128)(2,1)}, bf16[128,2048]{1,0:T(8,128)(2,1)S(1)}, u32[]{:S(2)}, u32[]{:S(2)}) collective-permute-start(bf16[128,2048]{1,0:T(8,128)(2,1)} %get-tuple-element.13), channel_id=1, source_target_pairs={{0,2},{1,3},{2,0},{3,1},{4,6},{5,7},{6,4},{7,5},{8,10},{9,11},{10,... | collective-permute-start | bytes 1572872 | tf_op jit(solution)/shard_map/ppermute | solution.py:21
  10.9 23.7 %collective-permute-start = (bf16[128,2048]{1,0:T(8,128)(2,1)}, bf16[128,2048]{1,0:T(8,128)(2,1)S(1)}, u32[]{:S(2)}, u32[]{:S(2)}) collective-permute-start(bf16[128,2048]{1,0:T(8,128)(2,1)} %get-tuple-element.14), channel_id=1, source_target_pairs={{0,1},{1,0},{2,3},{3,2},{4,5},{5,4},{6,7},{7,6},{8,9},{9,8},{10,11... | collective-permute-start | bytes 1572872 | tf_op jit(solution)/shard_map/ppermute | solution.py:21
  12.5 3.8 %copy-start = (bf16[2048,1024]{1,0:T(8,128)(2,1)S(1)}, bf16[2048,1024]{1,0:T(8,128)(2,1)}, u32[]{:S(2)}) copy-start(bf16[2048,1024]{1,0:T(8,128)(2,1)} %param.5) | copy-start | bytes 12582916
  19.9 34.4 %collective-permute-start.11 = (bf16[256,1024]{1,0:T(8,128)(2,1)S(1)}, bf16[256,1024]{1,0:T(8,128)(2,1)S(1)}, u32[]{:S(2)}, u32[]{:S(2)}) collective-permute-start(bf16[256,1024]{1,0:T(8,128)(2,1)S(1)} %constant_dynamic-update-slice_fusion.4), channel_id=1, source_target_pairs={{0,4},{4,0},{8,12},{12,8},{16,20},{20,16},{24,28},{28,24},{1,5},{5... | collective-permute-start | bytes 1572872 | tf_op jit(solution)/shard_map/ppermute | solution.py:35
  20.0 32.2 %collective-permute-start.12 = (bf16[256,1024]{1,0:T(8,128)(2,1)S(1)}, bf16[256,1024]{1,0:T(8,128)(2,1)S(1)}, u32[]{:S(2)}, u32[]{:S(2)}) collective-permute-start(bf16[256,1024]{1,0:T(8,128)(2,1)S(1)} %constant_dynamic-update-slice_fusion.4), channel_id=1, source_target_pairs={{0,8},{4,12},{8,0},{12,4},{16,24},{20,28},{24,16},{28,20},{1,9},{5... | collective-permute-start | bytes 1572872 | tf_op jit(solution)/shard_map/ppermute | solution.py:35
  21.6 6.0 %copy-start.1 = (bf16[2048,1024]{1,0:T(8,128)(2,1)S(1)}, bf16[2048,1024]{1,0:T(8,128)(2,1)}, u32[]{:S(2)}) copy-start(bf16[2048,1024]{1,0:T(8,128)(2,1)} %param.5) | copy-start | bytes 12582916
  22.2 7.2 %copy-start.2 = (bf16[2048,1024]{1,0:T(8,128)(2,1)S(1)}, bf16[2048,1024]{1,0:T(8,128)(2,1)}, u32[]{:S(2)}) copy-start(bf16[2048,1024]{1,0:T(8,128)(2,1)} %param.6) | copy-start | bytes 12582916
  25.0 28.6 %collective-permute-start.13 = (bf16[256,1024]{1,0:T(8,128)(2,1)S(1)}, bf16[256,1024]{1,0:T(8,128)(2,1)S(1)}, u32[]{:S(2)}, u32[]{:S(2)}) collective-permute-start(bf16[256,1024]{1,0:T(8,128)(2,1)S(1)} %constant_dynamic-update-slice_fusion.4), channel_id=1, source_target_pairs={{0,16},{4,20},{8,24},{12,28},{16,0},{20,4},{24,8},{28,12},{1,17},{... | collective-permute-start | bytes 1572872 | tf_op jit(solution)/shard_map/ppermute | solution.py:35
  34.7 32.7 %collective-permute-start.17 = (bf16[256,1024]{1,0:T(8,128)(2,1)S(1)}, bf16[256,1024]{1,0:T(8,128)(2,1)S(1)}, u32[]{:S(2)}, u32[]{:S(2)}) collective-permute-start(bf16[256,1024]{1,0:T(8,128)(2,1)S(1)} %constant_dynamic-update-slice_fusion.4), channel_id=1, source_target_pairs={{8,16},{12,20},{16,8},{20,12},{9,17},{13,21},{17,9},{21,13},{10,18... | collective-permute-start | bytes 1572872 | tf_op jit(solution)/shard_map/ppermute | solution.py:35
  36.1 8.1 %collective-permute-start.4 = (bf16[128,1024]{1,0:T(8,128)(2,1)S(1)}, bf16[128,1024]{1,0:T(8,128)(2,1)S(1)}, u32[]{:S(2)}, u32[]{:S(2)}) collective-permute-start(bf16[128,1024]{1,0:T(8,128)(2,1)S(1)} %convolution_convert_fusion.7), channel_id=1, source_target_pairs={{0,1},{1,0},{2,3},{3,2},{4,5},{5,4},{6,7},{7,6},{8,9},{9,8},{10,11... | collective-permute-start | bytes 786440 | tf_op jit(solution)/shard_map/ppermute | solution.py:21
  44.2 7.2 %collective-permute-start.7 = (bf16[128,1024]{1,0:T(8,128)(2,1)S(1)}, bf16[128,1024]{1,0:T(8,128)(2,1)S(1)}, u32[]{:S(2)}, u32[]{:S(2)}) collective-permute-start(bf16[128,1024]{1,0:T(8,128)(2,1)S(1)} %convolution_convert_fusion.5), channel_id=1, source_target_pairs={{0,2},{1,3},{2,0},{3,1},{4,6},{5,7},{6,4},{7,5},{8,10},{9,11},{10,... | collective-permute-start | bytes 786440 | tf_op jit(solution)/shard_map/ppermute | solution.py:21
  51.4 9.1 %collective-permute-start.1 = (bf16[128,1024]{1,0:T(8,128)(2,1)S(1)}, bf16[128,1024]{1,0:T(8,128)(2,1)S(1)}, u32[]{:S(2)}, u32[]{:S(2)}) collective-permute-start(bf16[128,1024]{1,0:T(8,128)(2,1)S(1)} %convolution_convert_fusion.8), channel_id=1, source_target_pairs={{0,1},{1,0},{2,3},{3,2},{4,5},{5,4},{6,7},{7,6},{8,9},{9,8},{10,11... | collective-permute-start | bytes 786440 | tf_op jit(solution)/shard_map/ppermute | solution.py:21
  52.2 13.3 %copy-start.6 = (f32[128,1024]{1,0:T(8,128)S(1)}, f32[128,1024]{1,0:T(8,128)}, u32[]{:S(2)}) copy-start(f32[128,1024]{1,0:T(8,128)} %fusion.15) | copy-start | bytes 1572868
  52.2 13.3 %copy-start.7 = (f32[128,1024]{1,0:T(8,128)S(1)}, f32[128,1024]{1,0:T(8,128)}, u32[]{:S(2)}) copy-start(f32[128,1024]{1,0:T(8,128)} %fusion.17) | copy-start | bytes 1572868
  52.2 9.2 %collective-permute-start.6 = (bf16[128,1024]{1,0:T(8,128)(2,1)S(1)}, bf16[128,1024]{1,0:T(8,128)(2,1)S(1)}, u32[]{:S(2)}, u32[]{:S(2)}) collective-permute-start(bf16[128,1024]{1,0:T(8,128)(2,1)S(1)} %convolution_convert_fusion.6), channel_id=1, source_target_pairs={{0,2},{1,3},{2,0},{3,1},{4,6},{5,7},{6,4},{7,5},{8,10},{9,11},{10,... | collective-permute-start | bytes 786440 | tf_op jit(solution)/shard_map/ppermute | solution.py:21
  53.6 10.6 %collective-permute-start.5 = (bf16[128,1024]{1,0:T(8,128)(2,1)S(1)}, bf16[128,1024]{1,0:T(8,128)(2,1)S(1)}, u32[]{:S(2)}, u32[]{:S(2)}) collective-permute-start(bf16[128,1024]{1,0:T(8,128)(2,1)S(1)} %fusion.13), channel_id=1, source_target_pairs={{0,2},{1,3},{2,0},{3,1},{4,6},{5,7},{6,4},{7,5},{8,10},{9,11},{10,... | collective-permute-start | bytes 786440 | tf_op jit(solution)/shard_map/ppermute | solution.py:21
  54.3 11.2 %collective-permute-start.8 = (bf16[128,1024]{1,0:T(8,128)(2,1)S(1)}, bf16[128,1024]{1,0:T(8,128)(2,1)S(1)}, u32[]{:S(2)}, u32[]{:S(2)}) collective-permute-start(bf16[128,1024]{1,0:T(8,128)(2,1)S(1)} %fusion.14), channel_id=1, source_target_pairs={{0,1},{1,0},{2,3},{3,2},{4,5},{5,4},{6,7},{7,6},{8,9},{9,8},{10,11... | collective-permute-start | bytes 786440 | tf_op jit(solution)/shard_map/ppermute | solution.py:21
  56.5 10.1 %copy-start.3 = (bf16[1024,2048]{1,0:T(8,128)(2,1)S(1)}, bf16[1024,2048]{1,0:T(8,128)(2,1)}, u32[]{:S(2)}) copy-start(bf16[1024,2048]{1,0:T(8,128)(2,1)} %param.7) | copy-start | bytes 12582916
  60.6 20.8 %collective-permute-start.14 = (bf16[256,1024]{1,0:T(8,128)(2,1)S(1)}, bf16[256,1024]{1,0:T(8,128)(2,1)S(1)}, u32[]{:S(2)}, u32[]{:S(2)}) collective-permute-start(bf16[256,1024]{1,0:T(8,128)(2,1)S(1)} %collective-permute-done.12), channel_id=1, source_target_pairs={{0,4},{4,0},{8,12},{12,8},{16,20},{20,16},{24,28},{28,24},{1,5},{5... | collective-permute-start | bytes 1572872 | tf_op jit(solution)/shard_map/ppermute | solution.py:35
  61.4 20.0 %collective-permute-start.15 = (bf16[256,1024]{1,0:T(8,128)(2,1)S(1)}, bf16[256,1024]{1,0:T(8,128)(2,1)S(1)}, u32[]{:S(2)}, u32[]{:S(2)}) collective-permute-start(bf16[256,1024]{1,0:T(8,128)(2,1)S(1)} %collective-permute-done.13), channel_id=1, source_target_pairs={{0,4},{4,0},{8,12},{12,8},{16,20},{20,16},{24,28},{28,24},{1,5},{5... | collective-permute-start | bytes 1572872 | tf_op jit(solution)/shard_map/ppermute | solution.py:35
  64.2 13.9 %collective-permute-start.16 = (bf16[256,1024]{1,0:T(8,128)(2,1)S(1)}, bf16[256,1024]{1,0:T(8,128)(2,1)S(1)}, u32[]{:S(2)}, u32[]{:S(2)}) collective-permute-start(bf16[256,1024]{1,0:T(8,128)(2,1)S(1)} %collective-permute-done.13), channel_id=1, source_target_pairs={{16,24},{20,28},{8,0},{12,4},{17,25},{21,29},{9,1},{13,5},{18,26},... | collective-permute-start | bytes 1572872 | tf_op jit(solution)/shard_map/ppermute | solution.py:35
  65.9 12.4 %collective-permute-start.19 = (bf16[128,1024]{1,0:T(8,128)(2,1)S(1)}, bf16[128,1024]{1,0:T(8,128)(2,1)S(1)}, u32[]{:S(2)}, u32[]{:S(2)}) collective-permute-start(bf16[128,1024]{1,0:T(8,128)(2,1)S(1)} %multiply_convert_fusion), channel_id=1, source_target_pairs={{0,2},{1,3},{2,0},{3,1},{4,5},{5,4},{6,7},{7,6},{8,10},{9,11},{10,... | collective-permute-start | bytes 786440 | tf_op jit(solution)/shard_map/ppermute | solution.py:31
  67.4 12.3 %collective-permute-start.21 = (bf16[128,1024]{1,0:T(8,128)(2,1)S(1)}, bf16[128,1024]{1,0:T(8,128)(2,1)S(1)}, u32[]{:S(2)}, u32[]{:S(2)}) collective-permute-start(bf16[128,1024]{1,0:T(8,128)(2,1)S(1)} %multiply_convert_fusion), channel_id=1, source_target_pairs={{0,1},{1,0},{2,3},{3,2},{4,6},{5,7},{6,4},{7,5},{8,9},{9,8},{10,11... | collective-permute-start | bytes 786440 | tf_op jit(solution)/shard_map/ppermute | solution.py:31
  78.2 3.4 %collective-permute-start.18 = (bf16[256,1024]{1,0:T(8,128)(2,1)S(1)}, bf16[256,1024]{1,0:T(8,128)(2,1)S(1)}, u32[]{:S(2)}, u32[]{:S(2)}) collective-permute-start(bf16[256,1024]{1,0:T(8,128)(2,1)S(1)} %broadcast_select_fusion), channel_id=1, source_target_pairs={{0,4},{4,0},{8,12},{12,8},{16,20},{20,16},{24,28},{28,24},{1,5},{5... | collective-permute-start | bytes 1572872 | tf_op jit(solution)/shard_map/ppermute | solution.py:35
  78.8 7.7 %collective-permute-start.20 = (bf16[128,1024]{1,0:T(8,128)(2,1)S(1)}, bf16[128,1024]{1,0:T(8,128)(2,1)S(1)}, u32[]{:S(2)}, u32[]{:S(2)}) collective-permute-start(bf16[128,1024]{1,0:T(8,128)(2,1)S(1)} %fusion.5), channel_id=1, source_target_pairs={{0,2},{1,3},{2,0},{3,1},{4,5},{5,4},{6,7},{7,6},{8,10},{9,11},{10,... | collective-permute-start | bytes 786440 | tf_op jit(solution)/shard_map/ppermute | solution.py:31
  80.2 9.2 %collective-permute-start.22 = (bf16[128,1024]{1,0:T(8,128)(2,1)S(1)}, bf16[128,1024]{1,0:T(8,128)(2,1)S(1)}, u32[]{:S(2)}, u32[]{:S(2)}) collective-permute-start(bf16[128,1024]{1,0:T(8,128)(2,1)S(1)} %fusion.8), channel_id=1, source_target_pairs={{0,1},{1,0},{2,3},{3,2},{4,6},{5,7},{6,4},{7,5},{8,9},{9,8},{10,11... | collective-permute-start | bytes 786440 | tf_op jit(solution)/shard_map/ppermute | solution.py:31
  82.1 10.0 %collective-permute-start.23 = (bf16[128,1024]{1,0:T(8,128)(2,1)S(1)}, bf16[128,1024]{1,0:T(8,128)(2,1)S(1)}, u32[]{:S(2)}, u32[]{:S(2)}) collective-permute-start(bf16[128,1024]{1,0:T(8,128)(2,1)S(1)} %convolution_convert_fusion.2), channel_id=1, source_target_pairs={{0,2},{1,3},{2,0},{3,1},{4,5},{5,4},{6,7},{7,6},{8,10},{9,11},{10,... | collective-permute-start | bytes 786440 | tf_op jit(solution)/shard_map/ppermute | solution.py:31
  84.3 8.8 %collective-permute-start.24 = (bf16[128,1024]{1,0:T(8,128)(2,1)S(1)}, bf16[128,1024]{1,0:T(8,128)(2,1)S(1)}, u32[]{:S(2)}, u32[]{:S(2)}) collective-permute-start(bf16[128,1024]{1,0:T(8,128)(2,1)S(1)} %convolution_convert_fusion.1), channel_id=1, source_target_pairs={{0,1},{1,0},{2,3},{3,2},{4,6},{5,7},{6,4},{7,5},{8,9},{9,8},{10,11... | collective-permute-start | bytes 786440 | tf_op jit(solution)/shard_map/ppermute | solution.py:31
  (1 other events, 1.3 us)

commit v2 on v1

--- a/solution.py
+++ b/solution.py
@@ -107,7 +107,7 @@
         if turned:
             if line:
                 relayed = send_dp(two, [(2, 3), (1, 0)], 0)
-                late.append((jnp.where((chip == 0) | (chip == chips - 1), relayed, middle), chip ^ 3))
+                late.append(((relayed, middle), chip ^ 3))
             far_b = {a: jnp.zeros((hidden_width, half), jnp.bfloat16) for a in range(1, rows)}
             far_a = {b: jnp.zeros((hidden_width, half), jnp.bfloat16) for b in range(1, rows)}
 
@@ -144,7 +144,9 @@
         for a, other in near_a.items():
             give(other, w_a, (a, 0), (-a, 0), at_a)
         if turned:
-            tied, _ = lax.optimization_barrier(([p for p, _ in late], hidden))
+            tied, _ = lax.optimization_barrier(([p for p, _ in late], near_b))
+            if line:
+                tied = [jnp.where((chip == 0) | (chip == chips - 1), *tied[0])]
             fill([(p, at) for p, (_, at) in zip(tied, late)])
         for b, other in near_b.items():
             for a in far_b:

time: 94.7 us -> 94.7 us (level)
    ppermute x8, waiting for transfers between devices: 9.18 us -> 3.83 us  [send_dp(): return lax.ppermute(x, 'dp', pairs)]
    ppermute x6, waiting for transfers between devices: 7.44 us -> 12.8 us  [send_turned(): return lax.ppermute(x, ('dp', 'row', 'col'), pairs)]
  transfers between devices with their start and end apart: 25 -> 25, of which waited for: 12 -> 13; matrix products, arithmetic and copies ran while one was open for 23% -> 23% of each run, Pallas kernels for 0% -> 0%
where the time goes in v2:
time: 94.7 us; the launch traced here: 94.2 us
  waiting for transfers between devices  42.6 us (45%)
  starting transfers between devices  26.7 us (28%)
  matrix products  15.4 us (16%)
  local copies, waits for them, and re-layouts  8.72 us (9%)
    ppermute x11, waiting for transfers between devices, send(): return lax.ppermute(x, ('row', 'col'), pairs)  25.9 us
    dot_general x15, matrix products, matmul(): return jnp.dot(x, y, preferred_element_type=jnp.float32)  15.4 us
    ppermute x11, starting transfers between devices, send(): return lax.ppermute(x, ('row', 'col'), pairs)  13.9 us
    ppermute x6, waiting for transfers between devices, send_turned(): return lax.ppermute(x, ('dp', 'row', 'col'), pairs)  12.8 us
    ppermute x6, starting transfers between devices, send_turned(): return lax.ppermute(x, ('dp', 'row', 'col'), pairs)  6.47 us
    ppermute x8, starting transfers between devices, send_dp(): return lax.ppermute(x, 'dp', pairs)  6.33 us
    ppermute x8, waiting for transfers between devices, send_dp(): return lax.ppermute(x, 'dp', pairs)  3.83 us
    dynamic_slice x1, local copies, waits for them, and re-layouts, columns(): return lax.dynamic_slice_in_dim(x, at, size, axis=1)  2.57 us
  transfers between devices with their start and end apart: 25, of which 13 were waited for; matrix products, arithmetic and copies ran while one was open for 23% of the time, Pallas kernels for 0%

profile of v2, /device:TPU:0, one launch (start us, length us, event | category | flops | bytes accessed | tf_op | source)
XLA Modules:
  0.0 94.2 jit_solution(11686507735735340095)
XLA Ops:
  0.0 1.9 %fusion.23 = (bf16[128,1024]{1,0:T(8,128)(2,1)S(1)}, bf16[128,1024]{1,0:T(8,128)(2,1)}) fusion(bf16[1024,2048]{1,0:T(8,128)(2,1)} %param.7, s32[]{:T(128)S(6)} %select_n.181, s32[]{:T(128)S(6)} %add.386), kind=kLoop, calls=%fused_computation.58 | loop fusion | bytes 1048584 | tf_op jit(solution)/shard_map/slice | solution.py:64
  1.9 3.0 %collective-permute-start.9 = (bf16[128,1024]{1,0:T(8,128)(2,1)}, bf16[128,1024]{1,0:T(8,128)(2,1)}, u32[]{:S(2)}, u32[]{:S(2)}) collective-permute-start(bf16[128,1024]{1,0:T(8,128)(2,1)} %get-tuple-element.14), channel_id=1, source_target_pairs={{0,1},{1,0},{2,3},{3,2},{4,5},{5,4},{6,7},{7,6},{8,9},{9,8},{10,11... | collective-permute-start | bytes 786440 | tf_op jit(solution)/shard_map/ppermute | solution.py:21
  4.9 1.5 %collective-permute-start.10 = (bf16[128,1024]{1,0:T(8,128)(2,1)S(1)}, bf16[128,1024]{1,0:T(8,128)(2,1)}, u32[]{:S(2)}, u32[]{:S(2)}) collective-permute-start(bf16[128,1024]{1,0:T(8,128)(2,1)S(1)} %get-tuple-element.13), channel_id=1, source_target_pairs={{0,2},{1,3},{2,0},{3,1},{4,6},{5,7},{6,4},{7,5},{8,10},{9,11},{10,... | collective-permute-start | bytes 786440 | tf_op jit(solution)/shard_map/ppermute | solution.py:21
  6.4 2.6 %constant_dynamic-slice_fusion.2 = (bf16[128,2048]{1,0:T(8,128)(2,1)}, bf16[128,2048]{1,0:T(8,128)(2,1)}, bf16[128,2048]{1,0:T(8,128)(2,1)}) fusion(bf16[128,8192]{1,0:T(8,128)(2,1)} %param.4, s32[]{:T(128)S(6)} %select_n.179, s32[]{:T(128)S(6)} %select_n.177, s32[]{:T(128)S(6)} %select_n.180), kind=kLoop, calls=%fused_computation.55 | loop fusion | bytes 3145740 | tf_op jit(solution)/shard_map/dynamic_slice | solution.py:56
  9.0 2.0 %collective-permute-start.2 = (bf16[128,2048]{1,0:T(8,128)(2,1)}, bf16[128,2048]{1,0:T(8,128)(2,1)S(1)}, u32[]{:S(2)}, u32[]{:S(2)}) collective-permute-start(bf16[128,2048]{1,0:T(8,128)(2,1)} %get-tuple-element.15), channel_id=1, source_target_pairs={{0,2},{1,3},{2,0},{3,1},{4,6},{5,7},{6,4},{7,5},{8,10},{9,11},{10,... | collective-permute-start | bytes 1572872 | tf_op jit(solution)/shard_map/ppermute | solution.py:21
  10.9 1.5 %collective-permute-start = (bf16[128,2048]{1,0:T(8,128)(2,1)}, bf16[128,2048]{1,0:T(8,128)(2,1)S(1)}, u32[]{:S(2)}, u32[]{:S(2)}) collective-permute-start(bf16[128,2048]{1,0:T(8,128)(2,1)} %get-tuple-element.16), channel_id=1, source_target_pairs={{0,1},{1,0},{2,3},{3,2},{4,5},{5,4},{6,7},{7,6},{8,9},{9,8},{10,11... | collective-permute-start | bytes 1572872 | tf_op jit(solution)/shard_map/ppermute | solution.py:21
  12.5 3.8 %fusion.15 = f32[128,1024]{1,0:T(8,128)} fusion(bf16[2048,1024]{1,0:T(8,128)(2,1)} %param.6, bf16[128,8192]{1,0:T(8,128)(2,1)S(1)} %copy-done.4, s32[]{:T(128)S(6)} %select_n.175), kind=kOutput, calls=%fused_computation.24 | convolution fusion | flops 536870912 | bytes 5242884 | tf_op jit(solution)/shard_map/dot_general | solution.py:38
  16.3 1.6 %fusion.17 = f32[128,1024]{1,0:T(8,128)} fusion(bf16[2048,1024]{1,0:T(8,128)(2,1)S(1)} %copy-done, bf16[128,8192]{1,0:T(8,128)(2,1)S(1)} %copy-done.4, s32[]{:T(128)S(6)} %select_n.175), kind=kOutput, calls=%fused_computation.26 | convolution fusion | flops 536870912 | bytes 5242884 | tf_op jit(solution)/shard_map/dot_general | solution.py:38
  17.9 1.0 %constant_dynamic-update-slice_fusion.5 = bf16[256,1024]{1,0:T(8,128)(2,1)S(1)} fusion(bf16[256,1024]{1,0:T(8,128)(2,1)S(1)} %broadcast_in_dim.7, bf16[128,1024]{1,0:T(8,128)(2,1)} %collective-permute-done.9, s32[]{:T(128)S(6)} %select_n.183), kind=kLoop, calls=%fused_computation.53 | loop fusion | bytes 524292 | tf_op jit(solution)/shard_map/dynamic_update_slice | solution.py:67
  18.9 1.0 %constant_dynamic-update-slice_fusion.4 = bf16[256,1024]{1,0:T(8,128)(2,1)S(1)} fusion(bf16[256,1024]{1,0:T(8,128)(2,1)S(1)} %constant_dynamic-update-slice_fusion.5, bf16[128,1024]{1,0:T(8,128)(2,1)} %collective-permute-done.10, s32[]{:T(128)S(6)} %select_n.184), kind=kLoop, calls=%fused_computation.52 | loop fusion | bytes 524292 | tf_op jit(solution)/shard_map/dynamic_update_slice | solution.py:68
  20.0 1.6 %collective-permute-start.12 = (bf16[256,1024]{1,0:T(8,128)(2,1)S(1)}, bf16[256,1024]{1,0:T(8,128)(2,1)S(1)}, u32[]{:S(2)}, u32[]{:S(2)}) collective-permute-start(bf16[256,1024]{1,0:T(8,128)(2,1)S(1)} %constant_dynamic-update-slice_fusion.4), channel_id=1, source_target_pairs={{0,8},{4,12},{8,0},{12,4},{16,24},{20,28},{24,16},{28,20},{1,9},{5... | collective-permute-start | bytes 1572872 | tf_op jit(solution)/shard_map/ppermute | solution.py:35
  22.2 2.8 %collective-permute-done.3 = bf16[128,2048]{1,0:T(8,128)(2,1)} collective-permute-done((bf16[128,2048]{1,0:T(8,128)(2,1)}, bf16[128,2048]{1,0:T(8,128)(2,1)}, u32[]{:S(2)}, u32[]{:S(2)}) %collective-permute-start.3) | collective-permute-done | bytes 524320 | tf_op jit(solution)/shard_map/ppermute | solution.py:21
  25.0 2.6 %collective-permute-start.13 = (bf16[256,1024]{1,0:T(8,128)(2,1)S(1)}, bf16[256,1024]{1,0:T(8,128)(2,1)S(1)}, u32[]{:S(2)}, u32[]{:S(2)}) collective-permute-start(bf16[256,1024]{1,0:T(8,128)(2,1)S(1)} %constant_dynamic-update-slice_fusion.4), channel_id=1, source_target_pairs={{0,16},{4,20},{8,24},{12,28},{16,0},{20,4},{24,8},{28,12},{1,17},{... | collective-permute-start | bytes 1572872 | tf_op jit(solution)/shard_map/ppermute | solution.py:35
  27.6 1.8 %convolution_convert_fusion.7 = bf16[128,1024]{1,0:T(8,128)(2,1)S(1)} fusion(bf16[128,2048]{1,0:T(8,128)(2,1)} %collective-permute-done.3, bf16[2048,1024]{1,0:T(8,128)(2,1)S(1)} %copy-done.1), kind=kOutput, calls=%fused_computation.20 | convolution fusion | flops 537001984 | bytes 4980736 | tf_op jit(solution)/shard_map/dot_general | solution.py:38
  29.4 1.8 %convolution_convert_fusion.5 = bf16[128,1024]{1,0:T(8,128)(2,1)S(1)} fusion(bf16[128,2048]{1,0:T(8,128)(2,1)} %collective-permute-done.3, bf16[2048,1024]{1,0:T(8,128)(2,1)S(1)} %copy-done.2), kind=kOutput, calls=%fused_computation.18 | convolution fusion | flops 537001984 | bytes 4980736 | tf_op jit(solution)/shard_map/dot_general | solution.py:38
  31.3 3.4 %collective-permute-done = bf16[128,2048]{1,0:T(8,128)(2,1)S(1)} collective-permute-done((bf16[128,2048]{1,0:T(8,128)(2,1)}, bf16[128,2048]{1,0:T(8,128)(2,1)S(1)}, u32[]{:S(2)}, u32[]{:S(2)}) %collective-permute-start) | collective-permute-done | bytes 524320 | tf_op jit(solution)/shard_map/ppermute | solution.py:21
  36.1 1.2 %collective-permute-start.4 = (bf16[128,1024]{1,0:T(8,128)(2,1)S(1)}, bf16[128,1024]{1,0:T(8,128)(2,1)S(1)}, u32[]{:S(2)}, u32[]{:S(2)}) collective-permute-start(bf16[128,1024]{1,0:T(8,128)(2,1)S(1)} %convolution_convert_fusion.7), channel_id=1, source_target_pairs={{0,1},{1,0},{2,3},{3,2},{4,5},{5,4},{6,7},{7,6},{8,9},{9,8},{10,11... | collective-permute-start | bytes 786440 | tf_op jit(solution)/shard_map/ppermute | solution.py:21
  38.1 6.1 %collective-permute-done.4 = bf16[128,1024]{1,0:T(8,128)(2,1)S(1)} collective-permute-done((bf16[128,1024]{1,0:T(8,128)(2,1)S(1)}, bf16[128,1024]{1,0:T(8,128)(2,1)S(1)}, u32[]{:S(2)}, u32[]{:S(2)}) %collective-permute-start.4) | collective-permute-done | bytes 262176 | tf_op jit(solution)/shard_map/ppermute | solution.py:21
  45.6 5.8 %collective-permute-done.7 = bf16[128,1024]{1,0:T(8,128)(2,1)S(1)} collective-permute-done((bf16[128,1024]{1,0:T(8,128)(2,1)S(1)}, bf16[128,1024]{1,0:T(8,128)(2,1)S(1)}, u32[]{:S(2)}, u32[]{:S(2)}) %collective-permute-start.7) | collective-permute-done | bytes 262176 | tf_op jit(solution)/shard_map/ppermute | solution.py:21
  52.2 1.4 %collective-permute-start.6 = (bf16[128,1024]{1,0:T(8,128)(2,1)S(1)}, bf16[128,1024]{1,0:T(8,128)(2,1)S(1)}, u32[]{:S(2)}, u32[]{:S(2)}) collective-permute-start(bf16[128,1024]{1,0:T(8,128)(2,1)S(1)} %convolution_convert_fusion.6), channel_id=1, source_target_pairs={{0,2},{1,3},{2,0},{3,1},{4,6},{5,7},{6,4},{7,5},{8,10},{9,11},{10,... | collective-permute-start | bytes 786440 | tf_op jit(solution)/shard_map/ppermute | solution.py:21
  54.3 2.0 %collective-permute-start.8 = (bf16[128,1024]{1,0:T(8,128)(2,1)S(1)}, bf16[128,1024]{1,0:T(8,128)(2,1)S(1)}, u32[]{:S(2)}, u32[]{:S(2)}) collective-permute-start(bf16[128,1024]{1,0:T(8,128)(2,1)S(1)} %fusion.14), channel_id=1, source_target_pairs={{0,1},{1,0},{2,3},{3,2},{4,5},{5,4},{6,7},{7,6},{8,9},{9,8},{10,11... | collective-permute-start | bytes 786440 | tf_op jit(solution)/shard_map/ppermute | solution.py:21
  56.5 4.0 %collective-permute-done.1 = bf16[128,1024]{1,0:T(8,128)(2,1)S(1)} collective-permute-done((bf16[128,1024]{1,0:T(8,128)(2,1)S(1)}, bf16[128,1024]{1,0:T(8,128)(2,1)S(1)}, u32[]{:S(2)}, u32[]{:S(2)}) %collective-permute-start.1) | collective-permute-done | bytes 262176 | tf_op jit(solution)/shard_map/ppermute | solution.py:21
  61.4 2.8 %collective-permute-done.5 = bf16[128,1024]{1,0:T(8,128)(2,1)S(1)} collective-permute-done((bf16[128,1024]{1,0:T(8,128)(2,1)S(1)}, bf16[128,1024]{1,0:T(8,128)(2,1)S(1)}, u32[]{:S(2)}, u32[]{:S(2)}) %collective-permute-start.5) | collective-permute-done | bytes 262176 | tf_op jit(solution)/shard_map/ppermute | solution.py:21
  64.2 1.3 %collective-permute-start.16 = (bf16[256,1024]{1,0:T(8,128)(2,1)S(1)}, bf16[256,1024]{1,0:T(8,128)(2,1)S(1)}, u32[]{:S(2)}, u32[]{:S(2)}) collective-permute-start(bf16[256,1024]{1,0:T(8,128)(2,1)S(1)} %collective-permute-done.13), channel_id=1, source_target_pairs={{16,24},{20,28},{8,0},{12,4},{17,25},{21,29},{9,1},{13,5},{18,26},... | collective-permute-start | bytes 1572872 | tf_op jit(solution)/shard_map/ppermute | solution.py:35
  67.4 1.6 %collective-permute-start.21 = (bf16[128,1024]{1,0:T(8,128)(2,1)S(1)}, bf16[128,1024]{1,0:T(8,128)(2,1)S(1)}, u32[]{:S(2)}, u32[]{:S(2)}) collective-permute-start(bf16[128,1024]{1,0:T(8,128)(2,1)S(1)} %multiply_convert_fusion), channel_id=1, source_target_pairs={{0,1},{1,0},{2,3},{3,2},{4,6},{5,7},{6,4},{7,5},{8,9},{9,8},{10,11... | collective-permute-start | bytes 786440 | tf_op jit(solution)/shard_map/ppermute | solution.py:31
  69.0 5.3 %collective-permute-done.18 = bf16[128,1024]{1,0:T(8,128)(2,1)S(1)} collective-permute-done((bf16[128,1024]{1,0:T(8,128)(2,1)S(1)}, bf16[128,1024]{1,0:T(8,128)(2,1)S(1)}, u32[]{:S(2)}, u32[]{:S(2)}) %collective-permute-start.18) | collective-permute-done | bytes 262176 | tf_op jit(solution)/shard_map/ppermute | solution.py:31
  74.3 3.8 %collective-permute-done.16 = bf16[256,1024]{1,0:T(8,128)(2,1)S(1)} collective-permute-done((bf16[256,1024]{1,0:T(8,128)(2,1)S(1)}, bf16[256,1024]{1,0:T(8,128)(2,1)S(1)}, u32[]{:S(2)}, u32[]{:S(2)}) %collective-permute-start.16) | collective-permute-done | bytes 524320 | tf_op jit(solution)/shard_map/ppermute | solution.py:35
  80.2 1.2 %collective-permute-start.22 = (bf16[128,1024]{1,0:T(8,128)(2,1)S(1)}, bf16[128,1024]{1,0:T(8,128)(2,1)S(1)}, u32[]{:S(2)}, u32[]{:S(2)}) collective-permute-start(bf16[128,1024]{1,0:T(8,128)(2,1)S(1)} %fusion.8), channel_id=1, source_target_pairs={{0,1},{1,0},{2,3},{3,2},{4,6},{5,7},{6,4},{7,5},{8,9},{9,8},{10,11... | collective-permute-start | bytes 786440 | tf_op jit(solution)/shard_map/ppermute | solution.py:31
  82.1 1.8 %collective-permute-start.23 = (bf16[128,1024]{1,0:T(8,128)(2,1)S(1)}, bf16[128,1024]{1,0:T(8,128)(2,1)S(1)}, u32[]{:S(2)}, u32[]{:S(2)}) collective-permute-start(bf16[128,1024]{1,0:T(8,128)(2,1)S(1)} %convolution_convert_fusion.2), channel_id=1, source_target_pairs={{0,2},{1,3},{2,0},{3,1},{4,5},{5,4},{6,7},{7,6},{8,10},{9,11},{10,... | collective-permute-start | bytes 786440 | tf_op jit(solution)/shard_map/ppermute | solution.py:31
  86.5 2.9 %collective-permute-done.22 = bf16[128,1024]{1,0:T(8,128)(2,1)S(1)} collective-permute-done((bf16[128,1024]{1,0:T(8,128)(2,1)S(1)}, bf16[128,1024]{1,0:T(8,128)(2,1)S(1)}, u32[]{:S(2)}, u32[]{:S(2)}) %collective-permute-start.22) | collective-permute-done | bytes 262176 | tf_op jit(solution)/shard_map/ppermute | solution.py:31
  89.4 2.7 %collective-permute-done.23 = bf16[128,1024]{1,0:T(8,128)(2,1)S(1)} collective-permute-done((bf16[128,1024]{1,0:T(8,128)(2,1)S(1)}, bf16[128,1024]{1,0:T(8,128)(2,1)S(1)}, u32[]{:S(2)}, u32[]{:S(2)}) %collective-permute-start.23) | collective-permute-done | bytes 262176 | tf_op jit(solution)/shard_map/ppermute | solution.py:31
  92.1 1.0 %collective-permute-done.24 = bf16[128,1024]{1,0:T(8,128)(2,1)S(1)} collective-permute-done((bf16[128,1024]{1,0:T(8,128)(2,1)S(1)}, bf16[128,1024]{1,0:T(8,128)(2,1)S(1)}, u32[]{:S(2)}, u32[]{:S(2)}) %collective-permute-start.24) | collective-permute-done | bytes 262176 | tf_op jit(solution)/shard_map/ppermute | solution.py:31
  (72 shorter events, 14.8 us)
Async XLA Ops:
  0.0 12.5 %copy-start.4 = (bf16[128,8192]{1,0:T(8,128)(2,1)S(1)}, bf16[128,8192]{1,0:T(8,128)(2,1)}, u32[]{:S(2)}) copy-start(bf16[128,8192]{1,0:T(8,128)(2,1)} %param.4) | copy-start | bytes 6291460
  1.9 16.0 %collective-permute-start.9 = (bf16[128,1024]{1,0:T(8,128)(2,1)}, bf16[128,1024]{1,0:T(8,128)(2,1)}, u32[]{:S(2)}, u32[]{:S(2)}) collective-permute-start(bf16[128,1024]{1,0:T(8,128)(2,1)} %get-tuple-element.14), channel_id=1, source_target_pairs={{0,1},{1,0},{2,3},{3,2},{4,5},{5,4},{6,7},{7,6},{8,9},{9,8},{10,11... | collective-permute-start | bytes 786440 | tf_op jit(solution)/shard_map/ppermute | solution.py:21
  4.9 14.0 %collective-permute-start.10 = (bf16[128,1024]{1,0:T(8,128)(2,1)S(1)}, bf16[128,1024]{1,0:T(8,128)(2,1)}, u32[]{:S(2)}, u32[]{:S(2)}) collective-permute-start(bf16[128,1024]{1,0:T(8,128)(2,1)S(1)} %get-tuple-element.13), channel_id=1, source_target_pairs={{0,2},{1,3},{2,0},{3,1},{4,6},{5,7},{6,4},{7,5},{8,10},{9,11},{10,... | collective-permute-start | bytes 786440 | tf_op jit(solution)/shard_map/ppermute | solution.py:21
  9.0 16.1 %collective-permute-start.3 = (bf16[128,2048]{1,0:T(8,128)(2,1)}, bf16[128,2048]{1,0:T(8,128)(2,1)}, u32[]{:S(2)}, u32[]{:S(2)}) collective-permute-start(bf16[128,2048]{1,0:T(8,128)(2,1)} %get-tuple-element.17), channel_id=1, source_target_pairs={{0,3},{1,2},{2,1},{3,0},{4,7},{5,6},{6,5},{7,4},{8,11},{9,10},{10,... | collective-permute-start | bytes 1572872 | tf_op jit(solution)/shard_map/ppermute | solution.py:21
  9.0 27.1 %collective-permute-start.2 = (bf16[128,2048]{1,0:T(8,128)(2,1)}, bf16[128,2048]{1,0:T(8,128)(2,1)S(1)}, u32[]{:S(2)}, u32[]{:S(2)}) collective-permute-start(bf16[128,2048]{1,0:T(8,128)(2,1)} %get-tuple-element.15), channel_id=1, source_target_pairs={{0,2},{1,3},{2,0},{3,1},{4,6},{5,7},{6,4},{7,5},{8,10},{9,11},{10,... | collective-permute-start | bytes 1572872 | tf_op jit(solution)/shard_map/ppermute | solution.py:21
  10.9 23.7 %collective-permute-start = (bf16[128,2048]{1,0:T(8,128)(2,1)}, bf16[128,2048]{1,0:T(8,128)(2,1)S(1)}, u32[]{:S(2)}, u32[]{:S(2)}) collective-permute-start(bf16[128,2048]{1,0:T(8,128)(2,1)} %get-tuple-element.16), channel_id=1, source_target_pairs={{0,1},{1,0},{2,3},{3,2},{4,5},{5,4},{6,7},{7,6},{8,9},{9,8},{10,11... | collective-permute-start | bytes 1572872 | tf_op jit(solution)/shard_map/ppermute | solution.py:21
  12.5 3.8 %copy-start = (bf16[2048,1024]{1,0:T(8,128)(2,1)S(1)}, bf16[2048,1024]{1,0:T(8,128)(2,1)}, u32[]{:S(2)}) copy-start(bf16[2048,1024]{1,0:T(8,128)(2,1)} %param.5) | copy-start | bytes 12582916
  19.9 34.4 %collective-permute-start.11 = (bf16[256,1024]{1,0:T(8,128)(2,1)S(1)}, bf16[256,1024]{1,0:T(8,128)(2,1)S(1)}, u32[]{:S(2)}, u32[]{:S(2)}) collective-permute-start(bf16[256,1024]{1,0:T(8,128)(2,1)S(1)} %constant_dynamic-update-slice_fusion.4), channel_id=1, source_target_pairs={{0,4},{4,0},{8,12},{12,8},{16,20},{20,16},{24,28},{28,24},{1,5},{5... | collective-permute-start | bytes 1572872 | tf_op jit(solution)/shard_map/ppermute | solution.py:35
  20.0 32.2 %collective-permute-start.12 = (bf16[256,1024]{1,0:T(8,128)(2,1)S(1)}, bf16[256,1024]{1,0:T(8,128)(2,1)S(1)}, u32[]{:S(2)}, u32[]{:S(2)}) collective-permute-start(bf16[256,1024]{1,0:T(8,128)(2,1)S(1)} %constant_dynamic-update-slice_fusion.4), channel_id=1, source_target_pairs={{0,8},{4,12},{8,0},{12,4},{16,24},{20,28},{24,16},{28,20},{1,9},{5... | collective-permute-start | bytes 1572872 | tf_op jit(solution)/shard_map/ppermute | solution.py:35
  21.6 6.0 %copy-start.1 = (bf16[2048,1024]{1,0:T(8,128)(2,1)S(1)}, bf16[2048,1024]{1,0:T(8,128)(2,1)}, u32[]{:S(2)}) copy-start(bf16[2048,1024]{1,0:T(8,128)(2,1)} %param.5) | copy-start | bytes 12582916
  22.2 7.2 %copy-start.2 = (bf16[2048,1024]{1,0:T(8,128)(2,1)S(1)}, bf16[2048,1024]{1,0:T(8,128)(2,1)}, u32[]{:S(2)}) copy-start(bf16[2048,1024]{1,0:T(8,128)(2,1)} %param.6) | copy-start | bytes 12582916
  25.0 28.6 %collective-permute-start.13 = (bf16[256,1024]{1,0:T(8,128)(2,1)S(1)}, bf16[256,1024]{1,0:T(8,128)(2,1)S(1)}, u32[]{:S(2)}, u32[]{:S(2)}) collective-permute-start(bf16[256,1024]{1,0:T(8,128)(2,1)S(1)} %constant_dynamic-update-slice_fusion.4), channel_id=1, source_target_pairs={{0,16},{4,20},{8,24},{12,28},{16,0},{20,4},{24,8},{28,12},{1,17},{... | collective-permute-start | bytes 1572872 | tf_op jit(solution)/shard_map/ppermute | solution.py:35
  34.7 32.7 %collective-permute-start.17 = (bf16[256,1024]{1,0:T(8,128)(2,1)S(1)}, bf16[256,1024]{1,0:T(8,128)(2,1)S(1)}, u32[]{:S(2)}, u32[]{:S(2)}) collective-permute-start(bf16[256,1024]{1,0:T(8,128)(2,1)S(1)} %constant_dynamic-update-slice_fusion.4), channel_id=1, source_target_pairs={{8,16},{12,20},{16,8},{20,12},{9,17},{13,21},{17,9},{21,13},{10,18... | collective-permute-start | bytes 1572872 | tf_op jit(solution)/shard_map/ppermute | solution.py:35
  36.1 8.1 %collective-permute-start.4 = (bf16[128,1024]{1,0:T(8,128)(2,1)S(1)}, bf16[128,1024]{1,0:T(8,128)(2,1)S(1)}, u32[]{:S(2)}, u32[]{:S(2)}) collective-permute-start(bf16[128,1024]{1,0:T(8,128)(2,1)S(1)} %convolution_convert_fusion.7), channel_id=1, source_target_pairs={{0,1},{1,0},{2,3},{3,2},{4,5},{5,4},{6,7},{7,6},{8,9},{9,8},{10,11... | collective-permute-start | bytes 786440 | tf_op jit(solution)/shard_map/ppermute | solution.py:21
  44.2 7.2 %collective-permute-start.7 = (bf16[128,1024]{1,0:T(8,128)(2,1)S(1)}, bf16[128,1024]{1,0:T(8,128)(2,1)S(1)}, u32[]{:S(2)}, u32[]{:S(2)}) collective-permute-start(bf16[128,1024]{1,0:T(8,128)(2,1)S(1)} %convolution_convert_fusion.5), channel_id=1, source_target_pairs={{0,2},{1,3},{2,0},{3,1},{4,6},{5,7},{6,4},{7,5},{8,10},{9,11},{10,... | collective-permute-start | bytes 786440 | tf_op jit(solution)/shard_map/ppermute | solution.py:21
  51.4 9.1 %collective-permute-start.1 = (bf16[128,1024]{1,0:T(8,128)(2,1)S(1)}, bf16[128,1024]{1,0:T(8,128)(2,1)S(1)}, u32[]{:S(2)}, u32[]{:S(2)}) collective-permute-start(bf16[128,1024]{1,0:T(8,128)(2,1)S(1)} %convolution_convert_fusion.8), channel_id=1, source_target_pairs={{0,1},{1,0},{2,3},{3,2},{4,5},{5,4},{6,7},{7,6},{8,9},{9,8},{10,11... | collective-permute-start | bytes 786440 | tf_op jit(solution)/shard_map/ppermute | solution.py:21
  52.2 13.3 %copy-start.6 = (f32[128,1024]{1,0:T(8,128)S(1)}, f32[128,1024]{1,0:T(8,128)}, u32[]{:S(2)}) copy-start(f32[128,1024]{1,0:T(8,128)} %fusion.15) | copy-start | bytes 1572868
  52.2 13.3 %copy-start.7 = (f32[128,1024]{1,0:T(8,128)S(1)}, f32[128,1024]{1,0:T(8,128)}, u32[]{:S(2)}) copy-start(f32[128,1024]{1,0:T(8,128)} %fusion.17) | copy-start | bytes 1572868
  52.2 9.2 %collective-permute-start.6 = (bf16[128,1024]{1,0:T(8,128)(2,1)S(1)}, bf16[128,1024]{1,0:T(8,128)(2,1)S(1)}, u32[]{:S(2)}, u32[]{:S(2)}) collective-permute-start(bf16[128,1024]{1,0:T(8,128)(2,1)S(1)} %convolution_convert_fusion.6), channel_id=1, source_target_pairs={{0,2},{1,3},{2,0},{3,1},{4,6},{5,7},{6,4},{7,5},{8,10},{9,11},{10,... | collective-permute-start | bytes 786440 | tf_op jit(solution)/shard_map/ppermute | solution.py:21
  53.6 10.6 %collective-permute-start.5 = (bf16[128,1024]{1,0:T(8,128)(2,1)S(1)}, bf16[128,1024]{1,0:T(8,128)(2,1)S(1)}, u32[]{:S(2)}, u32[]{:S(2)}) collective-permute-start(bf16[128,1024]{1,0:T(8,128)(2,1)S(1)} %fusion.13), channel_id=1, source_target_pairs={{0,2},{1,3},{2,0},{3,1},{4,6},{5,7},{6,4},{7,5},{8,10},{9,11},{10,... | collective-permute-start | bytes 786440 | tf_op jit(solution)/shard_map/ppermute | solution.py:21
  54.3 11.2 %collective-permute-start.8 = (bf16[128,1024]{1,0:T(8,128)(2,1)S(1)}, bf16[128,1024]{1,0:T(8,128)(2,1)S(1)}, u32[]{:S(2)}, u32[]{:S(2)}) collective-permute-start(bf16[128,1024]{1,0:T(8,128)(2,1)S(1)} %fusion.14), channel_id=1, source_target_pairs={{0,1},{1,0},{2,3},{3,2},{4,5},{5,4},{6,7},{7,6},{8,9},{9,8},{10,11... | collective-permute-start | bytes 786440 | tf_op jit(solution)/shard_map/ppermute | solution.py:21
  56.5 10.1 %copy-start.3 = (bf16[1024,2048]{1,0:T(8,128)(2,1)S(1)}, bf16[1024,2048]{1,0:T(8,128)(2,1)}, u32[]{:S(2)}) copy-start(bf16[1024,2048]{1,0:T(8,128)(2,1)} %param.7) | copy-start | bytes 12582916
  60.6 20.8 %collective-permute-start.14 = (bf16[256,1024]{1,0:T(8,128)(2,1)S(1)}, bf16[256,1024]{1,0:T(8,128)(2,1)S(1)}, u32[]{:S(2)}, u32[]{:S(2)}) collective-permute-start(bf16[256,1024]{1,0:T(8,128)(2,1)S(1)} %collective-permute-done.12), channel_id=1, source_target_pairs={{0,4},{4,0},{8,12},{12,8},{16,20},{20,16},{24,28},{28,24},{1,5},{5... | collective-permute-start | bytes 1572872 | tf_op jit(solution)/shard_map/ppermute | solution.py:35
  61.4 20.0 %collective-permute-start.15 = (bf16[256,1024]{1,0:T(8,128)(2,1)S(1)}, bf16[256,1024]{1,0:T(8,128)(2,1)S(1)}, u32[]{:S(2)}, u32[]{:S(2)}) collective-permute-start(bf16[256,1024]{1,0:T(8,128)(2,1)S(1)} %collective-permute-done.13), channel_id=1, source_target_pairs={{0,4},{4,0},{8,12},{12,8},{16,20},{20,16},{24,28},{28,24},{1,5},{5... | collective-permute-start | bytes 1572872 | tf_op jit(solution)/shard_map/ppermute | solution.py:35
  64.2 13.9 %collective-permute-start.16 = (bf16[256,1024]{1,0:T(8,128)(2,1)S(1)}, bf16[256,1024]{1,0:T(8,128)(2,1)S(1)}, u32[]{:S(2)}, u32[]{:S(2)}) collective-permute-start(bf16[256,1024]{1,0:T(8,128)(2,1)S(1)} %collective-permute-done.13), channel_id=1, source_target_pairs={{16,24},{20,28},{8,0},{12,4},{17,25},{21,29},{9,1},{13,5},{18,26},... | collective-permute-start | bytes 1572872 | tf_op jit(solution)/shard_map/ppermute | solution.py:35
  65.9 8.5 %collective-permute-start.18 = (bf16[128,1024]{1,0:T(8,128)(2,1)S(1)}, bf16[128,1024]{1,0:T(8,128)(2,1)S(1)}, u32[]{:S(2)}, u32[]{:S(2)}) collective-permute-start(bf16[128,1024]{1,0:T(8,128)(2,1)S(1)} %multiply_convert_fusion), channel_id=1, source_target_pairs={{0,2},{1,3},{2,0},{3,1},{4,5},{5,4},{6,7},{7,6},{8,10},{9,11},{10,... | collective-permute-start | bytes 786440 | tf_op jit(solution)/shard_map/ppermute | solution.py:31
  67.4 12.3 %collective-permute-start.21 = (bf16[128,1024]{1,0:T(8,128)(2,1)S(1)}, bf16[128,1024]{1,0:T(8,128)(2,1)S(1)}, u32[]{:S(2)}, u32[]{:S(2)}) collective-permute-start(bf16[128,1024]{1,0:T(8,128)(2,1)S(1)} %multiply_convert_fusion), channel_id=1, source_target_pairs={{0,1},{1,0},{2,3},{3,2},{4,6},{5,7},{6,4},{7,5},{8,9},{9,8},{10,11... | collective-permute-start | bytes 786440 | tf_op jit(solution)/shard_map/ppermute | solution.py:31
  78.2 3.3 %collective-permute-start.19 = (bf16[256,1024]{1,0:T(8,128)(2,1)S(1)}, bf16[256,1024]{1,0:T(8,128)(2,1)S(1)}, u32[]{:S(2)}, u32[]{:S(2)}) collective-permute-start(bf16[256,1024]{1,0:T(8,128)(2,1)S(1)} %broadcast_select_fusion), channel_id=1, source_target_pairs={{0,4},{4,0},{8,12},{12,8},{16,20},{20,16},{24,28},{28,24},{1,5},{5... | collective-permute-start | bytes 1572872 | tf_op jit(solution)/shard_map/ppermute | solution.py:35
  78.7 7.7 %collective-permute-start.20 = (bf16[128,1024]{1,0:T(8,128)(2,1)S(1)}, bf16[128,1024]{1,0:T(8,128)(2,1)S(1)}, u32[]{:S(2)}, u32[]{:S(2)}) collective-permute-start(bf16[128,1024]{1,0:T(8,128)(2,1)S(1)} %fusion.5), channel_id=1, source_target_pairs={{0,2},{1,3},{2,0},{3,1},{4,5},{5,4},{6,7},{7,6},{8,10},{9,11},{10,... | collective-permute-start | bytes 786440 | tf_op jit(solution)/shard_map/ppermute | solution.py:31
  80.2 9.2 %collective-permute-start.22 = (bf16[128,1024]{1,0:T(8,128)(2,1)S(1)}, bf16[128,1024]{1,0:T(8,128)(2,1)S(1)}, u32[]{:S(2)}, u32[]{:S(2)}) collective-permute-start(bf16[128,1024]{1,0:T(8,128)(2,1)S(1)} %fusion.8), channel_id=1, source_target_pairs={{0,1},{1,0},{2,3},{3,2},{4,6},{5,7},{6,4},{7,5},{8,9},{9,8},{10,11... | collective-permute-start | bytes 786440 | tf_op jit(solution)/shard_map/ppermute | solution.py:31
  82.1 10.0 %collective-permute-start.23 = (bf16[128,1024]{1,0:T(8,128)(2,1)S(1)}, bf16[128,1024]{1,0:T(8,128)(2,1)S(1)}, u32[]{:S(2)}, u32[]{:S(2)}) collective-permute-start(bf16[128,1024]{1,0:T(8,128)(2,1)S(1)} %convolution_convert_fusion.2), channel_id=1, source_target_pairs={{0,2},{1,3},{2,0},{3,1},{4,5},{5,4},{6,7},{7,6},{8,10},{9,11},{10,... | collective-permute-start | bytes 786440 | tf_op jit(solution)/shard_map/ppermute | solution.py:31
  84.3 8.8 %collective-permute-start.24 = (bf16[128,1024]{1,0:T(8,128)(2,1)S(1)}, bf16[128,1024]{1,0:T(8,128)(2,1)S(1)}, u32[]{:S(2)}, u32[]{:S(2)}) collective-permute-start(bf16[128,1024]{1,0:T(8,128)(2,1)S(1)} %convolution_convert_fusion.1), channel_id=1, source_target_pairs={{0,1},{1,0},{2,3},{3,2},{4,6},{5,7},{6,4},{7,5},{8,9},{9,8},{10,11... | collective-permute-start | bytes 786440 | tf_op jit(solution)/shard_map/ppermute | solution.py:31
  (1 other events, 1.3 us)

commit v3 on v2

--- a/solution.py
+++ b/solution.py
@@ -43,29 +43,19 @@
         slab = w_gate.shape[0]
         hidden_width, width = w_down.shape
         half = width // 2
-        at_b = core * half if turned else 0
-        at_a = half - at_b
 
         def place(dr, dc):
             return (r + dr) % rows * cols + (c + dc) % cols
-
-        def place_turned(a, b):
-            return place(b + core * (a - b), a + core * (b - a)) if turned else place(b, a)
 
         def columns(x, at, size):
             return lax.dynamic_slice_in_dim(x, at, size, axis=1)
 
         early, late = [], []
         if turned:
-            share = hidden_width // dp
-            block = (rows - 1) * share
-            piece = lax.dynamic_slice_in_dim(w_down, d * share, share, axis=0)
-            along_col = [send(piece[:, :half], (0, -dc)) for dc in range(1, cols)]
-            along_row = [send(piece[:, half:], (-dr, 0)) for dr in range(1, rows)]
-            held = jnp.zeros((2 * block, half), jnp.bfloat16)
-            for i in range(rows - 1):
-                held = lax.dynamic_update_slice_in_dim(held, along_col[i], core * block + i * share, axis=0)
-                held = lax.dynamic_update_slice_in_dim(held, along_row[i], (1 - core) * block + i * share, axis=0)
+            share = hidden_width // chips
+            piece = lax.dynamic_slice(w_down, (chip * share, core * half), (share, half))
+            held = [send_turned(piece, (-a, 0)) for a in range(1, rows)]
+            held = held[0] if len(held) == 1 else jnp.concatenate(held, axis=0)
 
         feats = {s: columns(tokens, place(*s) * slab, slab) for s in shifts}
         got = {s: send(feats[s], s) for s in away}
@@ -108,61 +98,61 @@
             if line:
                 relayed = send_dp(two, [(2, 3), (1, 0)], 0)
                 late.append(((relayed, middle), chip ^ 3))
-            far_b = {a: jnp.zeros((hidden_width, half), jnp.bfloat16) for a in range(1, rows)}
-            far_a = {b: jnp.zeros((hidden_width, half), jnp.bfloat16) for b in range(1, rows)}
+            far = jnp.zeros((2 * (rows - 1) * hidden_width, half), jnp.bfloat16)
 
-            def fill(pieces):
+            def fill(far, pieces):
                 for k in range(cores):
                     for moved, from_chip in pieces:
                         if k:
                             moved = send_dp(moved, [(z, z) for z in range(chips)], k)
-                        at = (from_chip * cores + core + k * (1 - 2 * core)) * share
-                        for i, far in enumerate([far_a, far_b] if k else [far_b, far_a]):
-                            for j in range(1, rows):
-                                lower = i * block + (j - 1) * share
-                                far[j] = lax.dynamic_update_slice_in_dim(far[j], moved[lower : lower + share], at, axis=0)
+                        group = core + k * (1 - 2 * core)
+                        for i in range(rows - 1):
+                            at = (group * (rows - 1) + i) * hidden_width + from_chip * share
+                            far = lax.dynamic_update_slice_in_dim(far, moved[i * share : (i + 1) * share], at, axis=0)
+                return far
 
-            fill([(held, chip)])
+            far = fill(far, [(held, chip)])
             tied, _ = lax.optimization_barrier(([p for p, _ in early], gate_passed + up_passed))
-            fill([(p, at) for p, (_, at) in zip(tied, early)])
-        else:
-            far_b = {a: send(w_down[:, :half], (0, -a)) for a in range(1, cols)}
-            far_a = {b: send(w_down[:, half:], (-b, 0)) for b in range(1, rows)}
+            far = fill(far, [(p, at) for p, (_, at) in zip(tied, early)])
 
-        near_b = {b: send_turned(hidden, (0, -b)) for b in far_a}
-        near_a = {a: send_turned(hidden, (-a, 0)) for a in far_b}
-        w_b, w_a = columns(w_down, at_b, half), columns(w_down, at_a, half)
+        near = {(dr, 0): send(hidden, (-dr, 0)) for dr in range(1, rows)}
+        near |= {(0, dc): send(hidden, (0, -dc)) for dc in range(1, cols)}
 
         outs = []
 
         def give(x, weight, shift, slab_from, at):
-            out = send_turned(matmul(x, weight).astype(jnp.bfloat16), shift)
-            outs.append((out, place_turned(*slab_from) * width + at))
-
-        for b, other in near_b.items():
-            give(other, w_b, (0, b), (0, -b), at_b)
-        for a, other in near_a.items():
-            give(other, w_a, (a, 0), (-a, 0), at_a)
-        if turned:
-            tied, _ = lax.optimization_barrier(([p for p, _ in late], near_b))
-            if line:
-                tied = [jnp.where((chip == 0) | (chip == chips - 1), *tied[0])]
-            fill([(p, at) for p, (_, at) in zip(tied, late)])
-        for b, other in near_b.items():
-            for a in far_b:
-                give(other, far_b[a], (0, b), (a, -b), at_b)
-        for a, other in near_a.items():
-            for b in far_a:
-                give(other, far_a[b], (a, 0), (-a, b), at_a)
+            out = send(matmul(x, weight).astype(jnp.bfloat16), shift)
+            outs.append((out, place(*slab_from) * width + at))
 
         def keep(weight):
             return matmul(hidden, weight).astype(jnp.bfloat16)
 
+        for (dr, dc), other in near.items():
+            weight, at = (w_down[:, :half], 0) if dr else (w_down[:, half:], half)
+            give(other, weight, (dr, dc), (-dr, -dc), at)
+        if turned:
+            tied, _ = lax.optimization_barrier(([p for p, _ in late], near))
+            if line:
+                tied = [jnp.where((chip == 0) | (chip == chips - 1), *tied[0])]
+            far = fill(far, [(p, at) for p, (_, at) in zip(tied, late)])
+            blocks = [far[i * hidden_width : (i + 1) * hidden_width] for i in range(2 * (rows - 1))]
+            far_col = {dc: blocks[dc - 1] for dc in range(1, cols)}
+            far_row = {dr: blocks[rows - 1 + dr - 1] for dr in range(1, rows)}
+        else:
+            far_col = {dc: send(w_down[:, :half], (0, -dc)) for dc in range(1, cols)}
+            far_row = {dr: send(w_down[:, half:], (-dr, 0)) for dr in range(1, rows)}
+        for (dr, dc), other in near.items():
+            for i in far_col if dr else far_row:
+                if dr:
+                    give(other, far_col[i], (dr, 0), (-dr, i), 0)
+                else:
+                    give(other, far_row[i], (0, dc), (i, -dc), half)
+
         landed = [(keep(w_down), place(0, 0) * width)]
-        for a in far_b:
-            landed.append((keep(far_b[a]), place_turned(a, 0) * width + at_b))
-        for b in far_a:
-            landed.append((keep(far_a[b]), place_turned(0, b) * width + at_a))
+        for dc in far_col:
+            landed.append((keep(far_col[dc]), place(0, dc) * width))
+        for dr in far_row:
+            landed.append((keep(far_row[dr]), place(dr, 0) * width + half))
         mixed = jnp.zeros((tokens.shape[0], width * rows * cols), jnp.bfloat16)
         for block, at in landed + outs:
             mixed = lax.dynamic_update_slice_in_dim(mixed, block, at, axis=1)

time: 94.7 us -> 108 us (1.14)
  waiting for transfers between devices: 42.6 us -> 48.7 us
  matrix products: 15.4 us -> 18.7 us
  starting transfers between devices: 26.7 us -> 29.2 us
  other arithmetic: 0.36 us -> 1.63 us
    ppermute x8, waiting for transfers between devices: 3.83 us -> 20.4 us  [send_dp(): return lax.ppermute(x, 'dp', pairs)]
    ppermute x6 -> x1, waiting for transfers between devices: 12.8 us -> 5.11 us  [send_turned(): return lax.ppermute(x, ('dp', 'row', 'col'), pairs)]
    ppermute x11 -> x15, starting transfers between devices: 13.9 us -> 19.9 us  [send(): return lax.ppermute(x, ('row', 'col'), pairs)]
    ppermute x6 -> x1, starting transfers between devices: 6.47 us -> 1.99 us  [send_turned(): return lax.ppermute(x, ('dp', 'row', 'col'), pairs)]
    dot_general x15, matrix products: 15.4 us -> 18.7 us  [matmul(): return jnp.dot(x, y, preferred_element_type=jnp.float32)]
    ppermute x11 -> x15, waiting for transfers between devices: 25.9 us -> 23.2 us  [send(): return lax.ppermute(x, ('row', 'col'), pairs)]
    slice x1 -> x0, local copies, waits for them, and re-layouts: 1.92 us -> none  [shards(): along_row = [send(piece[:, half:], (-dr, 0)) for dr in range(1, rows)]]
    dynamic_slice x0 -> x1, local copies, waits for them, and re-layouts: none -> 1.86 us  [shards(): lax.dynamic_slice(w_down, (chip * share, core * half), (share, half))]
  transfers between devices with their start and end apart: 25 -> 24, of which waited for: 13 -> 14; matrix products, arithmetic and copies ran while one was open for 23% -> 23% of each run, Pallas kernels for 0% -> 0%
where the time goes in v3:
time: 108 us
  waiting for transfers between devices  48.7 us (45%)
  starting transfers between devices  29.2 us (27%)
  matrix products  18.7 us (17%)
  local copies, waits for them, and re-layouts  8.85 us (8%)
  other arithmetic  1.63 us (2%)
    ppermute x15, waiting for transfers between devices, send(): return lax.ppermute(x, ('row', 'col'), pairs)  23.2 us
    ppermute x8, waiting for transfers between devices, send_dp(): return lax.ppermute(x, 'dp', pairs)  20.4 us
    ppermute x15, starting transfers between devices, send(): return lax.ppermute(x, ('row', 'col'), pairs)  19.9 us
    dot_general x15, matrix products, matmul(): return jnp.dot(x, y, preferred_element_type=jnp.float32)  18.7 us
    ppermute x8, starting transfers between devices, send_dp(): return lax.ppermute(x, 'dp', pairs)  7.29 us
    ppermute x1, waiting for transfers between devices, send_turned(): return lax.ppermute(x, ('dp', 'row', 'col'), pairs)  5.11 us
    dynamic_slice x1, local copies, waits for them, and re-layouts, columns(): return lax.dynamic_slice_in_dim(x, at, size, axis=1)  2.71 us
    dynamic_update_slice x7, local copies, waits for them, and re-layouts, fill(): lax.dynamic_update_slice_in_dim(far, moved[i * share:(i + 1) * share], at...  2.54 us
  transfers between devices with their start and end apart: 24, of which 14 were waited for; matrix products, arithmetic and copies ran while one was open for 23% of the time, Pallas kernels for 0%

profile of v3, /device:TPU:0, one launch (start us, length us, event | category | flops | bytes accessed | tf_op | source)
XLA Modules:
  0.0 107.6 jit_solution(5051295595790137109)
XLA Ops:
  0.0 2.7 %constant_dynamic-slice_fusion.1 = (bf16[128,2048]{1,0:T(8,128)(2,1)}, bf16[128,2048]{1,0:T(8,128)(2,1)}, bf16[128,2048]{1,0:T(8,128)(2,1)}) fusion(bf16[128,8192]{1,0:T(8,128)(2,1)} %param.4, s32[]{:T(128)S(6)} %select_n.140, s32[]{:T(128)S(6)} %select_n.138, s32[]{:T(128)S(6)} %select_n.141), kind=kLoop, calls=%fused_computation.50 | loop fusion | bytes 3145740 | tf_op jit(solution)/shard_map/dynamic_slice | solution.py:51
  2.7 3.9 %collective-permute-start.3 = (bf16[128,2048]{1,0:T(8,128)(2,1)}, bf16[128,2048]{1,0:T(8,128)(2,1)}, u32[]{:S(2)}, u32[]{:S(2)}) collective-permute-start(bf16[128,2048]{1,0:T(8,128)(2,1)} %get-tuple-element.17), channel_id=1, source_target_pairs={{0,3},{1,2},{2,1},{3,0},{4,7},{5,6},{6,5},{7,4},{8,11},{9,10},{10,... | collective-permute-start | bytes 1572872 | tf_op jit(solution)/shard_map/ppermute | solution.py:21
  7.2 1.9 %dynamic_slice.19 = bf16[256,1024]{1,0:T(8,128)(2,1)} dynamic-slice(bf16[1024,2048]{1,0:T(8,128)(2,1)} %param.7, s32[]{:T(128)S(6)} %select_n.143, s32[]{:T(128)S(6)} %select_n.145), dynamic_slice_sizes={256,1024} | dynamic-slice | bytes 1048580 | tf_op jit(solution)/shard_map/dynamic_slice | solution.py:56
  9.1 2.0 %collective-permute-start.9 = (bf16[256,1024]{1,0:T(8,128)(2,1)}, bf16[256,1024]{1,0:T(8,128)(2,1)}, u32[]{:S(2)}, u32[]{:S(2)}) collective-permute-start(bf16[256,1024]{1,0:T(8,128)(2,1)} %dynamic_slice.19), channel_id=1, source_target_pairs={{0,1},{1,0},{2,3},{3,2},{4,6},{5,7},{6,4},{7,5},{8,9},{9,8},{10,11... | collective-permute-start | bytes 1572872 | tf_op jit(solution)/shard_map/ppermute | solution.py:31
  11.1 3.9 %fusion.39 = f32[128,1024]{1,0:T(8,128)} fusion(bf16[2048,1024]{1,0:T(8,128)(2,1)} %param.6, bf16[128,8192]{1,0:T(8,128)(2,1)S(1)} %copy-done.3, s32[]{:T(128)S(6)} %select_n.136), kind=kOutput, calls=%fused_computation.32 | convolution fusion | flops 536870912 | bytes 5242884 | tf_op jit(solution)/shard_map/dot_general | solution.py:38
  14.9 4.8 %collective-permute-done.3 = bf16[128,2048]{1,0:T(8,128)(2,1)} collective-permute-done((bf16[128,2048]{1,0:T(8,128)(2,1)}, bf16[128,2048]{1,0:T(8,128)(2,1)}, u32[]{:S(2)}, u32[]{:S(2)}) %collective-permute-start.3) | collective-permute-done | bytes 524320 | tf_op jit(solution)/shard_map/ppermute | solution.py:21
  19.8 3.1 %convolution_convert_fusion.3 = bf16[128,1024]{1,0:T(8,128)(2,1)S(1)} fusion(bf16[128,2048]{1,0:T(8,128)(2,1)} %collective-permute-done.3, bf16[2048,1024]{1,0:T(8,128)(2,1)} %param.5), kind=kOutput, calls=%fused_computation.28 | convolution fusion | flops 537001984 | bytes 4980736 | tf_op jit(solution)/shard_map/dot_general | solution.py:38
  22.8 2.1 %collective-permute-start.4 = (bf16[128,1024]{1,0:T(8,128)(2,1)S(1)}, bf16[128,1024]{1,0:T(8,128)(2,1)S(1)}, u32[]{:S(2)}, u32[]{:S(2)}) collective-permute-start(bf16[128,1024]{1,0:T(8,128)(2,1)S(1)} %convolution_convert_fusion.3), channel_id=1, source_target_pairs={{0,1},{1,0},{2,3},{3,2},{4,5},{5,4},{6,7},{7,6},{8,9},{9,8},{10,11... | collective-permute-start | bytes 786440 | tf_op jit(solution)/shard_map/ppermute | solution.py:21
  24.9 1.8 %convolution_convert_fusion.1 = bf16[128,1024]{1,0:T(8,128)(2,1)S(1)} fusion(bf16[128,2048]{1,0:T(8,128)(2,1)} %collective-permute-done.3, bf16[2048,1024]{1,0:T(8,128)(2,1)S(1)} %copy-done), kind=kOutput, calls=%fused_computation.26 | convolution fusion | flops 537001984 | bytes 4980736 | tf_op jit(solution)/shard_map/dot_general | solution.py:38
  26.7 1.6 %collective-permute-start.7 = (bf16[128,1024]{1,0:T(8,128)(2,1)S(1)}, bf16[128,1024]{1,0:T(8,128)(2,1)S(1)}, u32[]{:S(2)}, u32[]{:S(2)}) collective-permute-start(bf16[128,1024]{1,0:T(8,128)(2,1)S(1)} %convolution_convert_fusion.1), channel_id=1, source_target_pairs={{0,2},{1,3},{2,0},{3,1},{4,6},{5,7},{6,4},{7,5},{8,10},{9,11},{10,... | collective-permute-start | bytes 786440 | tf_op jit(solution)/shard_map/ppermute | solution.py:21
  28.3 1.8 %collective-permute-done = bf16[128,2048]{1,0:T(8,128)(2,1)S(1)} collective-permute-done((bf16[128,2048]{1,0:T(8,128)(2,1)}, bf16[128,2048]{1,0:T(8,128)(2,1)S(1)}, u32[]{:S(2)}, u32[]{:S(2)}) %collective-permute-start) | collective-permute-done | bytes 524320 | tf_op jit(solution)/shard_map/ppermute | solution.py:21
  30.1 1.4 %convolution_convert_fusion.4 = bf16[128,1024]{1,0:T(8,128)(2,1)} fusion(bf16[128,2048]{1,0:T(8,128)(2,1)S(1)} %collective-permute-done, bf16[2048,1024]{1,0:T(8,128)(2,1)S(1)} %copy-done.1), kind=kOutput, calls=%fused_computation.29 | convolution fusion | flops 537001984 | bytes 4980736 | tf_op jit(solution)/shard_map/dot_general | solution.py:38
  31.6 1.7 %collective-permute-start.1 = (bf16[128,1024]{1,0:T(8,128)(2,1)}, bf16[128,1024]{1,0:T(8,128)(2,1)S(1)}, u32[]{:S(2)}, u32[]{:S(2)}) collective-permute-start(bf16[128,1024]{1,0:T(8,128)(2,1)} %convolution_convert_fusion.4), channel_id=1, source_target_pairs={{0,1},{1,0},{2,3},{3,2},{4,5},{5,4},{6,7},{7,6},{8,9},{9,8},{10,11... | collective-permute-start | bytes 786440 | tf_op jit(solution)/shard_map/ppermute | solution.py:21
  33.3 1.5 %convolution_convert_fusion.2 = bf16[128,1024]{1,0:T(8,128)(2,1)} fusion(bf16[128,2048]{1,0:T(8,128)(2,1)S(1)} %collective-permute-done.2, bf16[2048,1024]{1,0:T(8,128)(2,1)S(1)} %copy-done), kind=kOutput, calls=%fused_computation.27 | convolution fusion | flops 537001984 | bytes 4980736 | tf_op jit(solution)/shard_map/dot_general | solution.py:38
  34.7 1.5 %collective-permute-start.6 = (bf16[128,1024]{1,0:T(8,128)(2,1)}, bf16[128,1024]{1,0:T(8,128)(2,1)}, u32[]{:S(2)}, u32[]{:S(2)}) collective-permute-start(bf16[128,1024]{1,0:T(8,128)(2,1)} %convolution_convert_fusion.2), channel_id=1, source_target_pairs={{0,2},{1,3},{2,0},{3,1},{4,6},{5,7},{6,4},{7,5},{8,10},{9,11},{10,... | collective-permute-start | bytes 786440 | tf_op jit(solution)/shard_map/ppermute | solution.py:21
  36.2 5.1 %collective-permute-done.9 = bf16[256,1024]{1,0:T(8,128)(2,1)} collective-permute-done((bf16[256,1024]{1,0:T(8,128)(2,1)}, bf16[256,1024]{1,0:T(8,128)(2,1)}, u32[]{:S(2)}, u32[]{:S(2)}) %collective-permute-start.9) | collective-permute-done | bytes 524320 | tf_op jit(solution)/shard_map/ppermute | solution.py:31
  41.3 1.8 %collective-permute-start.11 = (bf16[256,1024]{1,0:T(8,128)(2,1)}, bf16[256,1024]{1,0:T(8,128)(2,1)S(1)}, u32[]{:S(2)}, u32[]{:S(2)}) collective-permute-start(bf16[256,1024]{1,0:T(8,128)(2,1)} %collective-permute-done.9), channel_id=1, source_target_pairs={{0,8},{4,12},{8,0},{12,4},{16,24},{20,28},{24,16},{28,20},{1,9},{5... | collective-permute-start | bytes 1572872 | tf_op jit(solution)/shard_map/ppermute | solution.py:35
  44.0 2.8 %collective-permute-start.12 = (bf16[256,1024]{1,0:T(8,128)(2,1)}, bf16[256,1024]{1,0:T(8,128)(2,1)S(1)}, u32[]{:S(2)}, u32[]{:S(2)}) collective-permute-start(bf16[256,1024]{1,0:T(8,128)(2,1)} %collective-permute-done.9), channel_id=1, source_target_pairs={{0,16},{4,20},{8,24},{12,28},{16,0},{20,4},{24,8},{28,12},{1,17},{... | collective-permute-start | bytes 1572872 | tf_op jit(solution)/shard_map/ppermute | solution.py:35
  46.8 1.4 %fusion.37 = bf16[128,1024]{1,0:T(8,128)(2,1)} fusion(bf16[128,2048]{1,0:T(8,128)(2,1)S(1)} %collective-permute-done.2, bf16[2048,1024]{1,0:T(8,128)(2,1)S(1)} %copy-done.1, bf16[128,1024]{1,0:T(8,128)(2,1)S(1)} %collective-permute-done.4), kind=kOutput, calls=%fused_computation.24 | convolution fusion | flops 537264128 | bytes 5242880 | tf_op jit(solution)/shard_map/dot_general | solution.py:38
  48.3 1.5 %fusion.38 = bf16[128,1024]{1,0:T(8,128)(2,1)} fusion(bf16[128,2048]{1,0:T(8,128)(2,1)S(1)} %collective-permute-done, bf16[2048,1024]{1,0:T(8,128)(2,1)S(1)} %copy-done, bf16[128,1024]{1,0:T(8,128)(2,1)S(1)} %collective-permute-done.7), kind=kOutput, calls=%fused_computation.25 | convolution fusion | flops 537264128 | bytes 5242880 | tf_op jit(solution)/shard_map/dot_general | solution.py:38
  49.7 14.6 %collective-permute-done.11 = bf16[256,1024]{1,0:T(8,128)(2,1)S(1)} collective-permute-done((bf16[256,1024]{1,0:T(8,128)(2,1)}, bf16[256,1024]{1,0:T(8,128)(2,1)S(1)}, u32[]{:S(2)}, u32[]{:S(2)}) %collective-permute-start.11) | collective-permute-done | bytes 524320 | tf_op jit(solution)/shard_map/ppermute | solution.py:35
  64.3 1.5 %collective-permute-start.5 = (bf16[128,1024]{1,0:T(8,128)(2,1)}, bf16[128,1024]{1,0:T(8,128)(2,1)}, u32[]{:S(2)}, u32[]{:S(2)}) collective-permute-start(bf16[128,1024]{1,0:T(8,128)(2,1)} %fusion.37), channel_id=1, source_target_pairs={{0,2},{1,3},{2,0},{3,1},{4,6},{5,7},{6,4},{7,5},{8,10},{9,11},{10,... | collective-permute-start | bytes 786440 | tf_op jit(solution)/shard_map/ppermute | solution.py:21
  71.6 1.8 %collective-permute-done.8 = bf16[128,1024]{1,0:T(8,128)(2,1)} collective-permute-done((bf16[128,1024]{1,0:T(8,128)(2,1)}, bf16[128,1024]{1,0:T(8,128)(2,1)}, u32[]{:S(2)}, u32[]{:S(2)}) %collective-permute-start.8) | collective-permute-done | bytes 262176 | tf_op jit(solution)/shard_map/ppermute | solution.py:21
  73.4 1.4 %multiply_convert_fusion = bf16[128,1024]{1,0:T(8,128)(2,1)S(1)} fusion(bf16[128,1024]{1,0:T(8,128)(2,1)} %collective-permute-done.8, f32[128,1024]{1,0:T(8,128)S(1)} %copy-done.5, bf16[128,1024]{1,0:T(8,128)(2,1)} %collective-permute-done.6, bf16[128,1024]{1,0:T(8,128)(2,1)} %collective-permute-done.5, f32[128,1024]{1,0:T(8,128)S(1)} %fusion.41, ...), kind=kLoop, calls=%fused_computation.30 | loop fusion | flops 1835008 | bytes 2359296 | tf_op jit(solution)/shard_map/convert_element_type | solution.py:95
  77.9 1.6 %collective-permute-start.18 = (bf16[128,1024]{1,0:T(8,128)(2,1)S(1)}, bf16[128,1024]{1,0:T(8,128)(2,1)S(1)}, u32[]{:S(2)}, u32[]{:S(2)}) collective-permute-start(bf16[128,1024]{1,0:T(8,128)(2,1)S(1)} %multiply_convert_fusion), channel_id=1, source_target_pairs={{0,2},{1,3},{2,0},{3,1},{4,6},{5,7},{6,4},{7,5},{8,10},{9,11},{10,... | collective-permute-start | bytes 786440 | tf_op jit(solution)/shard_map/ppermute | solution.py:21
  81.4 3.5 %collective-permute-done.18 = bf16[128,1024]{1,0:T(8,128)(2,1)S(1)} collective-permute-done((bf16[128,1024]{1,0:T(8,128)(2,1)S(1)}, bf16[128,1024]{1,0:T(8,128)(2,1)S(1)}, u32[]{:S(2)}, u32[]{:S(2)}) %collective-permute-start.18) | collective-permute-done | bytes 262176 | tf_op jit(solution)/shard_map/ppermute | solution.py:21
  84.9 4.9 %collective-permute-done.15 = bf16[256,1024]{1,0:T(8,128)(2,1)S(1)} collective-permute-done((bf16[256,1024]{1,0:T(8,128)(2,1)S(1)}, bf16[256,1024]{1,0:T(8,128)(2,1)S(1)}, u32[]{:S(2)}, u32[]{:S(2)}) %collective-permute-start.15) | collective-permute-done | bytes 524320 | tf_op jit(solution)/shard_map/ppermute | solution.py:35
  90.7 1.5 %collective-permute-start.20 = (bf16[128,1024]{1,0:T(8,128)(2,1)S(1)}, bf16[128,1024]{1,0:T(8,128)(2,1)S(1)}, u32[]{:S(2)}, u32[]{:S(2)}) collective-permute-start(bf16[128,1024]{1,0:T(8,128)(2,1)S(1)} %fusion.31), channel_id=1, source_target_pairs={{0,2},{1,3},{2,0},{3,1},{4,6},{5,7},{6,4},{7,5},{8,10},{9,11},{10,... | collective-permute-start | bytes 786440 | tf_op jit(solution)/shard_map/ppermute | solution.py:21
  97.4 2.6 %collective-permute-done.20 = bf16[128,1024]{1,0:T(8,128)(2,1)S(1)} collective-permute-done((bf16[128,1024]{1,0:T(8,128)(2,1)S(1)}, bf16[128,1024]{1,0:T(8,128)(2,1)S(1)}, u32[]{:S(2)}, u32[]{:S(2)}) %collective-permute-start.20) | collective-permute-done | bytes 262176 | tf_op jit(solution)/shard_map/ppermute | solution.py:21
  100.0 2.0 %collective-permute-done.21 = bf16[128,1024]{1,0:T(8,128)(2,1)S(1)} collective-permute-done((bf16[128,1024]{1,0:T(8,128)(2,1)S(1)}, bf16[128,1024]{1,0:T(8,128)(2,1)S(1)}, u32[]{:S(2)}, u32[]{:S(2)}) %collective-permute-start.21) | collective-permute-done | bytes 262176 | tf_op jit(solution)/shard_map/ppermute | solution.py:21
  102.0 3.1 %collective-permute-done.22 = bf16[128,1024]{1,0:T(8,128)(2,1)S(1)} collective-permute-done((bf16[128,1024]{1,0:T(8,128)(2,1)S(1)}, bf16[128,1024]{1,0:T(8,128)(2,1)S(1)}, u32[]{:S(2)}, u32[]{:S(2)}) %collective-permute-start.22) | collective-permute-done | bytes 262176 | tf_op jit(solution)/shard_map/ppermute | solution.py:21
  105.2 1.7 %collective-permute-done.23 = bf16[128,1024]{1,0:T(8,128)(2,1)S(1)} collective-permute-done((bf16[128,1024]{1,0:T(8,128)(2,1)S(1)}, bf16[128,1024]{1,0:T(8,128)(2,1)S(1)}, u32[]{:S(2)}, u32[]{:S(2)}) %collective-permute-start.23) | collective-permute-done | bytes 262176 | tf_op jit(solution)/shard_map/ppermute | solution.py:21
  (68 shorter events, 18.8 us)
Async XLA Ops:
  0.0 11.1 %copy-start.3 = (bf16[128,8192]{1,0:T(8,128)(2,1)S(1)}, bf16[128,8192]{1,0:T(8,128)(2,1)}, u32[]{:S(2)}) copy-start(bf16[128,8192]{1,0:T(8,128)(2,1)} %param.4) | copy-start | bytes 6291460
  2.7 17.1 %collective-permute-start.3 = (bf16[128,2048]{1,0:T(8,128)(2,1)}, bf16[128,2048]{1,0:T(8,128)(2,1)}, u32[]{:S(2)}, u32[]{:S(2)}) collective-permute-start(bf16[128,2048]{1,0:T(8,128)(2,1)} %get-tuple-element.17), channel_id=1, source_target_pairs={{0,3},{1,2},{2,1},{3,0},{4,7},{5,6},{6,5},{7,4},{8,11},{9,10},{10,... | collective-permute-start | bytes 1572872 | tf_op jit(solution)/shard_map/ppermute | solution.py:21
  6.6 26.6 %collective-permute-start.2 = (bf16[128,2048]{1,0:T(8,128)(2,1)}, bf16[128,2048]{1,0:T(8,128)(2,1)S(1)}, u32[]{:S(2)}, u32[]{:S(2)}) collective-permute-start(bf16[128,2048]{1,0:T(8,128)(2,1)} %get-tuple-element.15), channel_id=1, source_target_pairs={{0,2},{1,3},{2,0},{3,1},{4,6},{5,7},{6,4},{7,5},{8,10},{9,11},{10,... | collective-permute-start | bytes 1572872 | tf_op jit(solution)/shard_map/ppermute | solution.py:21
  7.2 22.9 %collective-permute-start = (bf16[128,2048]{1,0:T(8,128)(2,1)}, bf16[128,2048]{1,0:T(8,128)(2,1)S(1)}, u32[]{:S(2)}, u32[]{:S(2)}) collective-permute-start(bf16[128,2048]{1,0:T(8,128)(2,1)} %get-tuple-element.16), channel_id=1, source_target_pairs={{0,1},{1,0},{2,3},{3,2},{4,5},{5,4},{6,7},{7,6},{8,9},{9,8},{10,11... | collective-permute-start | bytes 1572872 | tf_op jit(solution)/shard_map/ppermute | solution.py:21
  9.1 32.3 %collective-permute-start.9 = (bf16[256,1024]{1,0:T(8,128)(2,1)}, bf16[256,1024]{1,0:T(8,128)(2,1)}, u32[]{:S(2)}, u32[]{:S(2)}) collective-permute-start(bf16[256,1024]{1,0:T(8,128)(2,1)} %dynamic_slice.19), channel_id=1, source_target_pairs={{0,1},{1,0},{2,3},{3,2},{4,6},{5,7},{6,4},{7,5},{8,9},{9,8},{10,11... | collective-permute-start | bytes 1572872 | tf_op jit(solution)/shard_map/ppermute | solution.py:31
  11.1 13.8 %copy-start = (bf16[2048,1024]{1,0:T(8,128)(2,1)S(1)}, bf16[2048,1024]{1,0:T(8,128)(2,1)}, u32[]{:S(2)}) copy-start(bf16[2048,1024]{1,0:T(8,128)(2,1)} %param.6) | copy-start | bytes 12582916
  14.9 15.2 %copy-start.1 = (bf16[2048,1024]{1,0:T(8,128)(2,1)S(1)}, bf16[2048,1024]{1,0:T(8,128)(2,1)}, u32[]{:S(2)}) copy-start(bf16[2048,1024]{1,0:T(8,128)(2,1)} %param.5) | copy-start | bytes 12582916
  22.8 21.2 %collective-permute-start.4 = (bf16[128,1024]{1,0:T(8,128)(2,1)S(1)}, bf16[128,1024]{1,0:T(8,128)(2,1)S(1)}, u32[]{:S(2)}, u32[]{:S(2)}) collective-permute-start(bf16[128,1024]{1,0:T(8,128)(2,1)S(1)} %convolution_convert_fusion.3), channel_id=1, source_target_pairs={{0,1},{1,0},{2,3},{3,2},{4,5},{5,4},{6,7},{7,6},{8,9},{9,8},{10,11... | collective-permute-start | bytes 786440 | tf_op jit(solution)/shard_map/ppermute | solution.py:21
  26.7 21.6 %collective-permute-start.7 = (bf16[128,1024]{1,0:T(8,128)(2,1)S(1)}, bf16[128,1024]{1,0:T(8,128)(2,1)S(1)}, u32[]{:S(2)}, u32[]{:S(2)}) collective-permute-start(bf16[128,1024]{1,0:T(8,128)(2,1)S(1)} %convolution_convert_fusion.1), channel_id=1, source_target_pairs={{0,2},{1,3},{2,0},{3,1},{4,6},{5,7},{6,4},{7,5},{8,10},{9,11},{10,... | collective-permute-start | bytes 786440 | tf_op jit(solution)/shard_map/ppermute | solution.py:21
  31.6 38.6 %collective-permute-start.1 = (bf16[128,1024]{1,0:T(8,128)(2,1)}, bf16[128,1024]{1,0:T(8,128)(2,1)S(1)}, u32[]{:S(2)}, u32[]{:S(2)}) collective-permute-start(bf16[128,1024]{1,0:T(8,128)(2,1)} %convolution_convert_fusion.4), channel_id=1, source_target_pairs={{0,1},{1,0},{2,3},{3,2},{4,5},{5,4},{6,7},{7,6},{8,9},{9,8},{10,11... | collective-permute-start | bytes 786440 | tf_op jit(solution)/shard_map/ppermute | solution.py:21
  34.7 36.3 %collective-permute-start.6 = (bf16[128,1024]{1,0:T(8,128)(2,1)}, bf16[128,1024]{1,0:T(8,128)(2,1)}, u32[]{:S(2)}, u32[]{:S(2)}) collective-permute-start(bf16[128,1024]{1,0:T(8,128)(2,1)} %convolution_convert_fusion.2), channel_id=1, source_target_pairs={{0,2},{1,3},{2,0},{3,1},{4,6},{5,7},{6,4},{7,5},{8,10},{9,11},{10,... | collective-permute-start | bytes 786440 | tf_op jit(solution)/shard_map/ppermute | solution.py:21
  41.3 23.0 %collective-permute-start.11 = (bf16[256,1024]{1,0:T(8,128)(2,1)}, bf16[256,1024]{1,0:T(8,128)(2,1)S(1)}, u32[]{:S(2)}, u32[]{:S(2)}) collective-permute-start(bf16[256,1024]{1,0:T(8,128)(2,1)} %collective-permute-done.9), channel_id=1, source_target_pairs={{0,8},{4,12},{8,0},{12,4},{16,24},{20,28},{24,16},{28,20},{1,9},{5... | collective-permute-start | bytes 1572872 | tf_op jit(solution)/shard_map/ppermute | solution.py:35
  44.0 22.6 %collective-permute-start.12 = (bf16[256,1024]{1,0:T(8,128)(2,1)}, bf16[256,1024]{1,0:T(8,128)(2,1)S(1)}, u32[]{:S(2)}, u32[]{:S(2)}) collective-permute-start(bf16[256,1024]{1,0:T(8,128)(2,1)} %collective-permute-done.9), channel_id=1, source_target_pairs={{0,16},{4,20},{8,24},{12,28},{16,0},{20,4},{24,8},{28,12},{1,17},{... | collective-permute-start | bytes 1572872 | tf_op jit(solution)/shard_map/ppermute | solution.py:35
  48.3 27.2 %collective-permute-start.10 = (bf16[256,1024]{1,0:T(8,128)(2,1)}, bf16[256,1024]{1,0:T(8,128)(2,1)}, u32[]{:S(2)}, u32[]{:S(2)}) collective-permute-start(bf16[256,1024]{1,0:T(8,128)(2,1)} %collective-permute-done.9), channel_id=1, source_target_pairs={{0,4},{4,0},{8,12},{12,8},{16,20},{20,16},{24,28},{28,24},{1,5},{5... | collective-permute-start | bytes 1572872 | tf_op jit(solution)/shard_map/ppermute | solution.py:35
  49.7 23.6 %copy-start.5 = (f32[128,1024]{1,0:T(8,128)S(1)}, f32[128,1024]{1,0:T(8,128)}, u32[]{:S(2)}) copy-start(f32[128,1024]{1,0:T(8,128)} %fusion.39) | copy-start | bytes 1572868
  64.3 2.4 %copy-start.6 = (bf16[256,1024]{1,0:T(8,128)(2,1)}, bf16[256,1024]{1,0:T(8,128)(2,1)S(1)}, u32[]{:S(2)}) copy-start(bf16[256,1024]{1,0:T(8,128)(2,1)S(1)} %collective-permute-done.11) | copy-start | bytes 1572868
  64.3 6.8 %collective-permute-start.5 = (bf16[128,1024]{1,0:T(8,128)(2,1)}, bf16[128,1024]{1,0:T(8,128)(2,1)}, u32[]{:S(2)}, u32[]{:S(2)}) collective-permute-start(bf16[128,1024]{1,0:T(8,128)(2,1)} %fusion.37), channel_id=1, source_target_pairs={{0,2},{1,3},{2,0},{3,1},{4,6},{5,7},{6,4},{7,5},{8,10},{9,11},{10,... | collective-permute-start | bytes 786440 | tf_op jit(solution)/shard_map/ppermute | solution.py:21
  66.7 6.7 %collective-permute-start.8 = (bf16[128,1024]{1,0:T(8,128)(2,1)}, bf16[128,1024]{1,0:T(8,128)(2,1)}, u32[]{:S(2)}, u32[]{:S(2)}) collective-permute-start(bf16[128,1024]{1,0:T(8,128)(2,1)} %fusion.38), channel_id=1, source_target_pairs={{0,1},{1,0},{2,3},{3,2},{4,5},{5,4},{6,7},{7,6},{8,9},{9,8},{10,11... | collective-permute-start | bytes 786440 | tf_op jit(solution)/shard_map/ppermute | solution.py:21
  68.2 2.8 %copy-start.7 = (bf16[256,1024]{1,0:T(8,128)(2,1)S(1)}, bf16[256,1024]{1,0:T(8,128)(2,1)}, u32[]{:S(2)}) copy-start(bf16[256,1024]{1,0:T(8,128)(2,1)} %copy-done.6) | copy-start | bytes 1572868
  68.2 2.9 %copy-start.9 = (bf16[256,1024]{1,0:T(8,128)(2,1)S(1)}, bf16[256,1024]{1,0:T(8,128)(2,1)}, u32[]{:S(2)}) copy-start(bf16[256,1024]{1,0:T(8,128)(2,1)} %copy-done.8) | copy-start | bytes 1572868
  68.9 10.8 %copy-start.2 = (bf16[1024,2048]{1,0:T(8,128)(2,1)S(1)}, bf16[1024,2048]{1,0:T(8,128)(2,1)}, u32[]{:S(2)}) copy-start(bf16[1024,2048]{1,0:T(8,128)(2,1)} %param.7) | copy-start | bytes 12582916
  70.2 7.7 %collective-permute-start.16 = (bf16[256,1024]{1,0:T(8,128)(2,1)}, bf16[256,1024]{1,0:T(8,128)(2,1)S(1)}, u32[]{:S(2)}, u32[]{:S(2)}) collective-permute-start(bf16[256,1024]{1,0:T(8,128)(2,1)} %collective-permute-done.9), channel_id=1, source_target_pairs={{8,16},{12,20},{16,8},{20,12},{9,17},{13,21},{17,9},{21,13},{10,18... | collective-permute-start | bytes 1572872 | tf_op jit(solution)/shard_map/ppermute | solution.py:35
  71.0 18.8 %collective-permute-start.13 = (bf16[256,1024]{1,0:T(8,128)(2,1)S(1)}, bf16[256,1024]{1,0:T(8,128)(2,1)S(1)}, u32[]{:S(2)}, u32[]{:S(2)}) collective-permute-start(bf16[256,1024]{1,0:T(8,128)(2,1)S(1)} %copy-done.7), channel_id=1, source_target_pairs={{0,4},{4,0},{8,12},{12,8},{16,20},{20,16},{24,28},{28,24},{1,5},{5... | collective-permute-start | bytes 1572872 | tf_op jit(solution)/shard_map/ppermute | solution.py:35
  71.1 18.8 %collective-permute-start.14 = (bf16[256,1024]{1,0:T(8,128)(2,1)S(1)}, bf16[256,1024]{1,0:T(8,128)(2,1)S(1)}, u32[]{:S(2)}, u32[]{:S(2)}) collective-permute-start(bf16[256,1024]{1,0:T(8,128)(2,1)S(1)} %copy-done.9), channel_id=1, source_target_pairs={{0,4},{4,0},{8,12},{12,8},{16,20},{20,16},{24,28},{28,24},{1,5},{5... | collective-permute-start | bytes 1572872 | tf_op jit(solution)/shard_map/ppermute | solution.py:35
  74.8 6.6 %collective-permute-start.17 = (bf16[128,1024]{1,0:T(8,128)(2,1)S(1)}, bf16[128,1024]{1,0:T(8,128)(2,1)S(1)}, u32[]{:S(2)}, u32[]{:S(2)}) collective-permute-start(bf16[128,1024]{1,0:T(8,128)(2,1)S(1)} %multiply_convert_fusion), channel_id=1, source_target_pairs={{0,1},{1,0},{2,3},{3,2},{4,5},{5,4},{6,7},{7,6},{8,9},{9,8},{10,11... | collective-permute-start | bytes 786440 | tf_op jit(solution)/shard_map/ppermute | solution.py:21
  75.4 14.4 %collective-permute-start.15 = (bf16[256,1024]{1,0:T(8,128)(2,1)S(1)}, bf16[256,1024]{1,0:T(8,128)(2,1)S(1)}, u32[]{:S(2)}, u32[]{:S(2)}) collective-permute-start(bf16[256,1024]{1,0:T(8,128)(2,1)S(1)} %copy-done.9), channel_id=1, source_target_pairs={{16,24},{20,28},{8,0},{12,4},{17,25},{21,29},{9,1},{13,5},{18,26},... | collective-permute-start | bytes 1572872 | tf_op jit(solution)/shard_map/ppermute | solution.py:35
  77.9 7.0 %collective-permute-start.18 = (bf16[128,1024]{1,0:T(8,128)(2,1)S(1)}, bf16[128,1024]{1,0:T(8,128)(2,1)S(1)}, u32[]{:S(2)}, u32[]{:S(2)}) collective-permute-start(bf16[128,1024]{1,0:T(8,128)(2,1)S(1)} %multiply_convert_fusion), channel_id=1, source_target_pairs={{0,2},{1,3},{2,0},{3,1},{4,6},{5,7},{6,4},{7,5},{8,10},{9,11},{10,... | collective-permute-start | bytes 786440 | tf_op jit(solution)/shard_map/ppermute | solution.py:21
  90.2 3.4 %collective-permute-start.19 = (bf16[256,1024]{1,0:T(8,128)(2,1)S(1)}, bf16[256,1024]{1,0:T(8,128)(2,1)S(1)}, u32[]{:S(2)}, u32[]{:S(2)}) collective-permute-start(bf16[256,1024]{1,0:T(8,128)(2,1)S(1)} %get-tuple-element.14), channel_id=1, source_target_pairs={{0,4},{4,0},{8,12},{12,8},{16,20},{20,16},{24,28},{28,24},{1,5},{5... | collective-permute-start | bytes 1572872 | tf_op jit(solution)/shard_map/ppermute | solution.py:35
  90.7 9.2 %collective-permute-start.20 = (bf16[128,1024]{1,0:T(8,128)(2,1)S(1)}, bf16[128,1024]{1,0:T(8,128)(2,1)S(1)}, u32[]{:S(2)}, u32[]{:S(2)}) collective-permute-start(bf16[128,1024]{1,0:T(8,128)(2,1)S(1)} %fusion.31), channel_id=1, source_target_pairs={{0,2},{1,3},{2,0},{3,1},{4,6},{5,7},{6,4},{7,5},{8,10},{9,11},{10,... | collective-permute-start | bytes 786440 | tf_op jit(solution)/shard_map/ppermute | solution.py:21
  92.7 9.2 %collective-permute-start.21 = (bf16[128,1024]{1,0:T(8,128)(2,1)S(1)}, bf16[128,1024]{1,0:T(8,128)(2,1)S(1)}, u32[]{:S(2)}, u32[]{:S(2)}) collective-permute-start(bf16[128,1024]{1,0:T(8,128)(2,1)S(1)} %fusion.34), channel_id=1, source_target_pairs={{0,1},{1,0},{2,3},{3,2},{4,5},{5,4},{6,7},{7,6},{8,9},{9,8},{10,11... | collective-permute-start | bytes 786440 | tf_op jit(solution)/shard_map/ppermute | solution.py:21
  94.1 11.0 %collective-permute-start.22 = (bf16[128,1024]{1,0:T(8,128)(2,1)S(1)}, bf16[128,1024]{1,0:T(8,128)(2,1)S(1)}, u32[]{:S(2)}, u32[]{:S(2)}) collective-permute-start(bf16[128,1024]{1,0:T(8,128)(2,1)S(1)} %fusion.19), channel_id=1, source_target_pairs={{0,2},{1,3},{2,0},{3,1},{4,6},{5,7},{6,4},{7,5},{8,10},{9,11},{10,... | collective-permute-start | bytes 786440 | tf_op jit(solution)/shard_map/ppermute | solution.py:21
  95.7 11.2 %collective-permute-start.23 = (bf16[128,1024]{1,0:T(8,128)(2,1)S(1)}, bf16[128,1024]{1,0:T(8,128)(2,1)S(1)}, u32[]{:S(2)}, u32[]{:S(2)}) collective-permute-start(bf16[128,1024]{1,0:T(8,128)(2,1)S(1)} %fusion.28), channel_id=1, source_target_pairs={{0,1},{1,0},{2,3},{3,2},{4,5},{5,4},{6,7},{7,6},{8,9},{9,8},{10,11... | collective-permute-start | bytes 786440 | tf_op jit(solution)/shard_map/ppermute | solution.py:21
  (2 other events, 2.5 us)
